TPU v7x, 512 devices: a whole 4x4x16 slice. The times are simulated.
512 devices in a mesh: row: 32 (over z, x_lo), col: 16 (over y, x_hi, core).
Axes of the slice: x: 4 (x_hi: 2, x_lo: 2; x = x_hi * 2 + x_lo), y: 4, z: 16, core: 2. Of those that a mesh axis runs over, the one named last changes fastest.
Arguments:
- grad: bfloat16 [262144, 1024], P(('row', 'col')), may hold values from -2500 to 2500
- left_root: bfloat16 [262144, 1024], P(('row', 'col')), may hold values from -0.051 to 3, as said below
- right_root: bfloat16 [262144, 1024], P(('row', 'col')), may hold values from -0.051 to 3, as said below
Outputs:
- update: bfloat16 [262144, 1024], P(('row', 'col'))
Inputs may be any that keep to these rules, and one draw needn't show every extreme that they name: `left_root`: each block L_b is symmetric and positive definite. `right_root`: each block R_b is symmetric and positive definite.
All inputs are finite; a program needn't handle non-finite values.
Results may differ from a plain program's by a relative error of at most 0.0049.
Values may be sent and summed in bfloat16 or wider, within the bound.
No kernel may reach another device: no remote copies, remote signals or barrier semaphores. Data moves between devices by JAX's collectives and lax.ppermute only.
A program may use at most 64 MiB of HBM per device.

v0:
```python
import functools

import jax
import jax.numpy as jnp
from jax import lax
from jax.sharding import Mesh
from jax.sharding import PartitionSpec as P

BLK = 1024
COL = ("col_0", "col_1", "col_2")
ROW_COL = ("row_0", "row_1", "col_0", "col_1", "col_2")
ROW = ("row_0", "row_1")


epsilon = 1e-06
clip_rms = 1.0


def partner(shard, axis, distance):
    return lax.ppermute(shard, axis, [(i, i ^ 1 << distance) for i in range(lax.axis_size(axis))])


def over_axes(shard, axes):
    return functools.reduce(lax.psum, axes, shard)


def apply_right(gradient_rows, own_start, other_start, rows_here, right_root, partner_right):
    own_cols = lax.dynamic_slice_in_dim(gradient_rows, own_start, rows_here, 1)
    other_cols = lax.dynamic_slice_in_dim(gradient_rows, other_start, rows_here, 1)
    applied = jnp.dot(own_cols, right_root, preferred_element_type=jnp.float32)
    applied = applied + jnp.dot(other_cols, partner_right, preferred_element_type=jnp.float32)
    return applied.astype(jnp.bfloat16)


def shards(grad, left_root, right_root):
    rows_here = grad.shape[0]
    parity = lax.axis_index(COL) % 2
    own_start = parity * rows_here
    other_start = (1 - parity) * rows_here
    partner_right = partner(right_root, COL, 0)
    right_applied = apply_right(grad, own_start, other_start, rows_here, right_root, partner_right)
    partner_rows = partner(right_applied, COL, 0)
    own_left = lax.dynamic_slice_in_dim(left_root, own_start, rows_here, 1)
    other_left = lax.dynamic_slice_in_dim(left_root, other_start, rows_here, 1)
    preconditioned = jnp.dot(own_left, right_applied, preferred_element_type=jnp.float32)
    preconditioned = preconditioned + jnp.dot(
        other_left, partner_rows, preferred_element_type=jnp.float32
    )
    grad_sq = jnp.sum(jnp.square(grad.astype(jnp.float32)))
    cond_sq = jnp.sum(preconditioned * preconditioned)
    global_sq = over_axes(grad_sq, ROW_COL)
    partner_sums = partner(jnp.stack([grad_sq, cond_sq]), COL, 0)
    block_grad = grad_sq + partner_sums[0]
    block_cond = cond_sq + partner_sums[1]
    block_count = BLK * BLK
    total_count = lax.axis_size(ROW) * lax.axis_size(COL) // 2 * block_count
    clip_factor = clip_rms / jnp.sqrt(global_sq / total_count + epsilon)
    graft_ratio = jnp.sqrt(
        (block_grad / block_count + epsilon) / (block_cond / block_count + epsilon)
    )
    return (clip_factor * graft_ratio * preconditioned).astype(jnp.bfloat16)


def solution(mesh):
    torus = Mesh(
        mesh.devices.reshape(16, 2, 4, 2, 2), ("row_0", "row_1", "col_0", "col_1", "col_2")
    )
    return jax.shard_map(
        shards,
        mesh=torus,
        in_specs=(P(ROW_COL, None), P(ROW_COL, None), P(ROW_COL, None)),
        out_specs=P(ROW_COL, None),
        check_vma=False,
    )
```

profile of v0, /device:TPU:1, one launch (start us, length us, event | category | flops | bytes accessed | tf_op | source)
XLA Modules:
  0.0 88.7 jit_solution(8485458253239033572)
XLA Ops:
  0.0 0.0 copy-start
  0.0 0.0 copy-start.1
  0.0 8.9 %collective-permute-start = (bf16[512,1024]{1,0:T(8,128)(2,1)}, bf16[512,1024]{1,0:T(8,128)(2,1)}, u32[]{:S(2)}, u32[]{:S(2)}) collective-permute-start(bf16[512,1024]{1,0:T(8,128)(2,1)} %param.5), channel_id=1, source_target_pairs={{0,1},{1,0},{2,3},{3,2},{4,5},{5,4},{6,7},{7,6},{8,9},{9,8},{10,11... | collective-permute-start | bytes 3145736 | tf_op jit(solution)/shard_map/ppermute | solution.py:20
  8.9 2.1 %fusion.2 = f32[512,1024]{1,0:T(8,128)S(1)} fusion(bf16[512,1024]{1,0:T(8,128)(2,1)} %param.5, bf16[512,1024]{1,0:T(8,128)(2,1)} %param.3, s32[]{:T(128)S(6)} %select_n.16), kind=kOutput, calls=%fused_computation.7 | convolution fusion | flops 536870912 | bytes 3670020 | tf_op jit(solution)/shard_map/dot_general | solution.py:30
  11.0 0.5 collective-permute-done
  11.5 0.0 copy-done.1
  11.5 1.9 %add_convert_fusion = bf16[512,1024]{1,0:T(8,128)(2,1)S(1)} fusion(f32[512,1024]{1,0:T(8,128)S(1)} %fusion.2, bf16[512,1024]{1,0:T(8,128)(2,1)} %collective-permute-done, bf16[512,1024]{1,0:T(8,128)(2,1)S(1)} %copy-done.1, s32[]{:T(128)S(6)} %select_n.17), kind=kOutput, calls=%fused_computation.2 | convolution fusion | flops 537919488 | bytes 4718596 | tf_op jit(solution)/shard_map/dot_general | solution.py:31
  13.4 2.3 %collective-permute-start.1 = (bf16[512,1024]{1,0:T(8,128)(2,1)S(1)}, bf16[512,1024]{1,0:T(8,128)(2,1)}, u32[]{:S(2)}, u32[]{:S(2)}) collective-permute-start(bf16[512,1024]{1,0:T(8,128)(2,1)S(1)} %add_convert_fusion), channel_id=1, source_target_pairs={{0,1},{1,0},{2,3},{3,2},{4,5},{5,4},{6,7},{7,6},{8,9},{9,8},{10,11... | collective-permute-start | bytes 3145736 | tf_op jit(solution)/shard_map/ppermute | solution.py:20
  15.7 1.2 %multiply_reduce_fusion.1 = f32[]{:T(128)} fusion(bf16[512,1024]{1,0:T(8,128)(2,1)S(1)} %copy-done.1), kind=kLoop, calls=%fused_computation.3 | loop fusion | flops 1572863 | bytes 1048580 | tf_op jit(solution)/shard_map/reduce_sum | solution.py:49
  17.0 24.5 %psum.35 = f32[]{:T(128)} all-reduce(f32[]{:T(128)} %multiply_reduce_fusion.1), channel_id=1, replica_groups=mesh['row_0'=16,'row_1'=2,'col_0'=4,'col_1'=2,'col_2'=2] {'row_0'}, use_global_device_ids=true, to_apply=%region_1.2 | all-reduce | flops 1 | bytes 8 | tf_op jit(solution)/shard_map/psum | solution.py:24
  41.5 4.4 %psum.36 = f32[]{:T(128)} all-reduce(f32[]{:T(128)} %psum.35), channel_id=1, replica_groups=mesh['row_0'=16,'row_1'=2,'col_0'=4,'col_1'=2,'col_2'=2] {'row_1'}, use_global_device_ids=true, to_apply=%region_2.3 | all-reduce | flops 1 | bytes 8 | tf_op jit(solution)/shard_map/psum | solution.py:24
  45.9 9.3 %psum.37 = f32[]{:T(128)} all-reduce(f32[]{:T(128)} %psum.36), channel_id=1, replica_groups=mesh['row_0'=16,'row_1'=2,'col_0'=4,'col_1'=2,'col_2'=2] {'col_0'}, use_global_device_ids=true, to_apply=%region_3.4 | all-reduce | flops 1 | bytes 8 | tf_op jit(solution)/shard_map/psum | solution.py:24
  55.2 5.9 %psum.38 = f32[]{:T(128)} all-reduce(f32[]{:T(128)} %psum.37), channel_id=1, replica_groups=mesh['row_0'=16,'row_1'=2,'col_0'=4,'col_1'=2,'col_2'=2] {'col_1'}, use_global_device_ids=true, to_apply=%region_4.5 | all-reduce | flops 1 | bytes 8 | tf_op jit(solution)/shard_map/psum | solution.py:24
  61.1 14.4 %psum.39 = f32[]{:T(128)} all-reduce(f32[]{:T(128)} %psum.38), channel_id=1, replica_groups=mesh['row_0'=16,'row_1'=2,'col_0'=4,'col_1'=2,'col_2'=2] {'col_2'}, use_global_device_ids=true, to_apply=%region_5.6 | all-reduce | flops 1 | bytes 8 | tf_op jit(solution)/shard_map/psum | solution.py:24
  76.2 0.0 copy-done
  76.2 0.7 fusion.4
  77.0 0.0 collective-permute-done.1
  77.0 2.7 %multiply_reduce_fusion = (f32[]{:T(128)}, f32[512,1024]{1,0:T(8,128)S(1)}) fusion(f32[512,1024]{1,0:T(8,128)S(1)} %fusion.4, bf16[512,1024]{1,0:T(8,128)(2,1)} %collective-permute-done.1, bf16[512,1024]{1,0:T(8,128)(2,1)S(1)} %copy-done, s32[]{:T(128)S(6)} %select_n.17), kind=kOutput, calls=%fused_computation.1 | convolution fusion | flops 538443776 | bytes 5767176 | tf_op jit(solution)/shard_map/dot_general | solution.py:46
  79.7 1.4 %pad_maximum_fusion = f32[2]{0:T(128)S(1)} fusion(f32[1]{0:T(128)} %bitcast.1, f32[1]{0:T(128)} %bitcast), kind=kLoop, calls=%fused_computation.15 | loop fusion | flops 2 | bytes 16 | tf_op jit(solution)/shard_map/stack | solution.py:52
  81.1 2.2 %collective-permute-start.2 = (f32[2]{0:T(128)S(1)}, f32[2]{0:T(128)S(1)}, u32[]{:S(2)}, u32[]{:S(2)}) collective-permute-start(f32[2]{0:T(128)S(1)} %pad_maximum_fusion), channel_id=1, source_target_pairs={{0,1},{1,0},{2,3},{3,2},{4,5},{5,4},{6,7},{7,6},{8,9},{9,8},{10,11... | collective-permute-start | bytes 32 | tf_op jit(solution)/shard_map/ppermute | solution.py:20
  83.3 0.8 collective-permute-done.2
  84.1 0.7 fusion.10
  87.5 1.2 %multiply_convert_fusion = bf16[512,1024]{1,0:T(8,128)(2,1)} fusion(f32[512,1024]{1,0:T(8,128)S(1)} %get-tuple-element.8, f32[]{:T(128)S(6)} %mul.29), kind=kLoop, calls=%fused_computation | loop fusion | flops 1048576 | bytes 3145732 | tf_op jit(solution)/shard_map/convert_element_type | solution.py:61
Async XLA Ops:
  0.0 76.2 %copy-start = (bf16[512,1024]{1,0:T(8,128)(2,1)S(1)}, bf16[512,1024]{1,0:T(8,128)(2,1)}, u32[]{:S(2)}) copy-start(bf16[512,1024]{1,0:T(8,128)(2,1)} %param.4) | copy-start | bytes 3145732
  0.0 11.5 %copy-start.1 = (bf16[512,1024]{1,0:T(8,128)(2,1)S(1)}, bf16[512,1024]{1,0:T(8,128)(2,1)}, u32[]{:S(2)}) copy-start(bf16[512,1024]{1,0:T(8,128)(2,1)} %param.3) | copy-start | bytes 3145732
  0.0 11.5 %collective-permute-start = (bf16[512,1024]{1,0:T(8,128)(2,1)}, bf16[512,1024]{1,0:T(8,128)(2,1)}, u32[]{:S(2)}, u32[]{:S(2)}) collective-permute-start(bf16[512,1024]{1,0:T(8,128)(2,1)} %param.5), channel_id=1, source_target_pairs={{0,1},{1,0},{2,3},{3,2},{4,5},{5,4},{6,7},{7,6},{8,9},{9,8},{10,11... | collective-permute-start | bytes 3145736 | tf_op jit(solution)/shard_map/ppermute | solution.py:20
  13.4 63.5 %collective-permute-start.1 = (bf16[512,1024]{1,0:T(8,128)(2,1)S(1)}, bf16[512,1024]{1,0:T(8,128)(2,1)}, u32[]{:S(2)}, u32[]{:S(2)}) collective-permute-start(bf16[512,1024]{1,0:T(8,128)(2,1)S(1)} %add_convert_fusion), channel_id=1, source_target_pairs={{0,1},{1,0},{2,3},{3,2},{4,5},{5,4},{6,7},{7,6},{8,9},{9,8},{10,11... | collective-permute-start | bytes 3145736 | tf_op jit(solution)/shard_map/ppermute | solution.py:20
  81.1 3.0 %collective-permute-start.2 = (f32[2]{0:T(128)S(1)}, f32[2]{0:T(128)S(1)}, u32[]{:S(2)}, u32[]{:S(2)}) collective-permute-start(f32[2]{0:T(128)S(1)} %pad_maximum_fusion), channel_id=1, source_target_pairs={{0,1},{1,0},{2,3},{3,2},{4,5},{5,4},{6,7},{7,6},{8,9},{9,8},{10,11... | collective-permute-start | bytes 32 | tf_op jit(solution)/shard_map/ppermute | solution.py:20
where the time goes:
time: 89.1 us; the launch traced here: 88.7 us
  blocking collectives  58.6 us (66%)
  starting transfers between devices  13.4 us (15%)
  matrix products  7.48 us (8%)
  other arithmetic  3.84 us (4%)
  between operations  3.46 us (4%)
  waiting for transfers between devices  1.27 us (1%)
    psum x5, blocking collectives, over_axes(): return functools.reduce(lax.psum, axes, shard)  58.6 us
    ppermute x3, starting transfers between devices, partner(): lax.ppermute(shard, axis, [(i, i ^ 1 << distance) for i in range(lax.axis...  13.4 us
    dot_general x1, matrix products, shards(): jnp.dot(other_left, partner_rows, preferred_element_type=jnp.float32)  2.7 us
    dot_general x1, matrix products, apply_right(): applied = jnp.dot(own_cols, right_root, preferred_element_type=jnp.float32)  2.1 us
    dot_general x1, matrix products, apply_right(): jnp.dot(other_cols, partner_right, preferred_element_type=jnp.float32)  1.95 us
  transfers between devices with their start and end apart: 3, of which 2 were waited for; matrix products, arithmetic and copies ran while one was open for 5% of the time, Pallas kernels for 0%

commit v1 on v0

--- a/solution.py
+++ b/solution.py
@@ -10,6 +10,8 @@
 COL = ("col_0", "col_1", "col_2")
 ROW_COL = ("row_0", "row_1", "col_0", "col_1", "col_2")
 ROW = ("row_0", "row_1")
+PLANE = ("row_1", "col_0", "col_1", "col_2")
+LINE = "row_0"
 
 
 epsilon = 1e-06
@@ -20,8 +22,15 @@
     return lax.ppermute(shard, axis, [(i, i ^ 1 << distance) for i in range(lax.axis_size(axis))])
 
 
-def over_axes(shard, axes):
-    return functools.reduce(lax.psum, axes, shard)
+def over_group(value, axes):
+    members = lax.axis_size(axes)
+    sent = jnp.full((members, 128), value)
+    heard = lax.all_to_all(sent, axes, 0, 0, tiled=True)
+    return jnp.sum(heard[:, 0])
+
+
+def over_axes(shard, groups):
+    return functools.reduce(over_group, groups, shard)
 
 
 def apply_right(gradient_rows, own_start, other_start, rows_here, right_root, partner_right):
@@ -48,7 +57,7 @@
     )
     grad_sq = jnp.sum(jnp.square(grad.astype(jnp.float32)))
     cond_sq = jnp.sum(preconditioned * preconditioned)
-    global_sq = over_axes(grad_sq, ROW_COL)
+    global_sq = over_axes(grad_sq, (PLANE, LINE))
     partner_sums = partner(jnp.stack([grad_sq, cond_sq]), COL, 0)
     block_grad = grad_sq + partner_sums[0]
     block_cond = cond_sq + partner_sums[1]

time: 89.1 us -> 69.5 us (0.78)
  blocking collectives: 58.6 us -> 34.6 us
  starting transfers between devices: 13.4 us -> 15.1 us
  local copies, waits for them, and re-layouts: 0.67 us -> 2.02 us
  other arithmetic: 3.84 us -> 5.05 us
    psum x5 -> x0, blocking collectives: 58.6 us -> none  [over_axes(): return functools.reduce(lax.psum, axes, shard)]
    all_to_all x0 -> x2, blocking collectives: none -> 34.6 us  [over_group(): heard = lax.all_to_all(sent, axes, 0, 0, tiled=True)]
    ppermute x3, starting transfers between devices: 13.4 us -> 15.1 us  [partner(): lax.ppermute(shard, axis, [(i, i ^ 1 << distance) for i in range(lax.axis...]
    broadcast_in_dim x0 -> x2, local copies, waits for them, and re-layouts: none -> 1.35 us  [over_group(): sent = jnp.full((members, 128), value)]
    reduce_sum x0 -> x2, other arithmetic: none -> 1.2 us  [over_group(): return jnp.sum(heard[:, 0])]
  transfers between devices with their start and end apart: 3 -> 3, of which waited for: 2 -> 2; matrix products, arithmetic and copies ran while one was open for 5% -> 10% of each run, Pallas kernels for 0% -> 0%
where the time goes in v1:
time: 69.5 us; the launch traced here: 69.1 us
  blocking collectives  34.6 us (50%)
  starting transfers between devices  15.1 us (22%)
  matrix products  7.48 us (11%)
  other arithmetic  5.05 us (7%)
  between operations  3.48 us (5%)
  local copies, waits for them, and re-layouts  2.02 us (3%)
  waiting for transfers between devices  1.27 us (2%)
    all_to_all x2, blocking collectives, over_group(): heard = lax.all_to_all(sent, axes, 0, 0, tiled=True)  34.6 us
    ppermute x3, starting transfers between devices, partner(): lax.ppermute(shard, axis, [(i, i ^ 1 << distance) for i in range(lax.axis...  15.1 us
    dot_general x1, matrix products, shards(): jnp.dot(other_left, partner_rows, preferred_element_type=jnp.float32)  2.7 us
    dot_general x1, matrix products, apply_right(): applied = jnp.dot(own_cols, right_root, preferred_element_type=jnp.float32)  2.1 us
    dot_general x1, matrix products, apply_right(): jnp.dot(other_cols, partner_right, preferred_element_type=jnp.float32)  1.95 us
    another operation x1, other arithmetic, shards(): partner_sums = partner(jnp.stack([grad_sq, cond_sq]), COL, 0)  1.41 us
  transfers between devices with their start and end apart: 3, of which 2 were waited for; matrix products, arithmetic and copies ran while one was open for 10% of the time, Pallas kernels for 0%

profile of v1, /device:TPU:1, one launch (start us, length us, event | category | flops | bytes accessed | tf_op | source)
XLA Modules:
  0.0 69.1 jit_solution(15835033521449404896)
XLA Ops:
  0.0 0.0 copy-start
  0.0 0.0 copy-start.1
  0.0 8.9 %collective-permute-start = (bf16[512,1024]{1,0:T(8,128)(2,1)}, bf16[512,1024]{1,0:T(8,128)(2,1)}, u32[]{:S(2)}, u32[]{:S(2)}) collective-permute-start(bf16[512,1024]{1,0:T(8,128)(2,1)} %param.5), channel_id=1, source_target_pairs={{0,1},{1,0},{2,3},{3,2},{4,5},{5,4},{6,7},{7,6},{8,9},{9,8},{10,11... | collective-permute-start | bytes 3145736 | tf_op jit(solution)/shard_map/ppermute | solution.py:22
  8.9 2.1 %fusion.2 = f32[512,1024]{1,0:T(8,128)S(1)} fusion(bf16[512,1024]{1,0:T(8,128)(2,1)} %param.5, bf16[512,1024]{1,0:T(8,128)(2,1)} %param.3, s32[]{:T(128)S(6)} %select_n.16), kind=kOutput, calls=%fused_computation.7 | convolution fusion | flops 536870912 | bytes 3670020 | tf_op jit(solution)/shard_map/dot_general | solution.py:39
  11.0 0.5 collective-permute-done
  11.5 0.0 copy-done.1
  11.5 1.9 %add_convert_fusion = bf16[512,1024]{1,0:T(8,128)(2,1)S(1)} fusion(f32[512,1024]{1,0:T(8,128)S(1)} %fusion.2, bf16[512,1024]{1,0:T(8,128)(2,1)} %collective-permute-done, bf16[512,1024]{1,0:T(8,128)(2,1)S(1)} %copy-done.1, s32[]{:T(128)S(6)} %select_n.17), kind=kOutput, calls=%fused_computation.2 | convolution fusion | flops 537919488 | bytes 4718596 | tf_op jit(solution)/shard_map/dot_general | solution.py:40
  13.4 2.3 %collective-permute-start.1 = (bf16[512,1024]{1,0:T(8,128)(2,1)S(1)}, bf16[512,1024]{1,0:T(8,128)(2,1)}, u32[]{:S(2)}, u32[]{:S(2)}) collective-permute-start(bf16[512,1024]{1,0:T(8,128)(2,1)S(1)} %add_convert_fusion), channel_id=1, source_target_pairs={{0,1},{1,0},{2,3},{3,2},{4,5},{5,4},{6,7},{7,6},{8,9},{9,8},{10,11... | collective-permute-start | bytes 3145736 | tf_op jit(solution)/shard_map/ppermute | solution.py:22
  15.7 1.2 %multiply_reduce_fusion.1 = f32[]{:T(128)} fusion(bf16[512,1024]{1,0:T(8,128)(2,1)S(1)} %copy-done.1), kind=kLoop, calls=%fused_computation.3 | loop fusion | flops 1572863 | bytes 1048580 | tf_op jit(solution)/shard_map/reduce_sum | solution.py:58
  17.0 0.7 %broadcast_in_dim.6 = f32[32,1,128]{2,1,0:T(1,128)S(1)} broadcast(f32[]{:T(128)} %multiply_reduce_fusion.1), dimensions={} | broadcast | bytes 16388 | tf_op jit(solution)/shard_map/broadcast_in_dim | solution.py:27
  17.7 9.7 %all_to_all.18 = f32[32,1,128]{2,1,0:T(1,128)S(1)} all-to-all(f32[32,1,128]{2,1,0:T(1,128)S(1)} %broadcast_in_dim.6), channel_id=1, replica_groups=mesh['row_0'=16,'row_1'=2,'col_0'=4,'col_1'=2,'col_2'=2] {'row_1','col_0..., dimensions={0} | all-to-all | bytes 32768 | tf_op jit(solution)/shard_map/all_to_all | solution.py:28
  27.4 0.6 slice_reduce_fusion
  28.0 0.6 broadcast_in_dim.7
  28.7 24.9 %all_to_all.19 = f32[16,1,128]{2,1,0:T(1,128)S(1)} all-to-all(f32[16,1,128]{2,1,0:T(1,128)S(1)} %broadcast_in_dim.7), channel_id=1, replica_groups=mesh['row_0'=16,'row_1'=2,'col_0'=4,'col_1'=2,'col_2'=2] {'row_0'}, dimensions={0} | all-to-all | bytes 16384 | tf_op jit(solution)/shard_map/all_to_all | solution.py:28
  53.6 0.6 slice_reduce_fusion.1
  54.9 0.0 copy-done
  54.9 0.7 %fusion.4 = f32[512,1024]{1,0:T(8,128)S(1)} fusion(bf16[512,1024]{1,0:T(8,128)(2,1)S(1)} %add_convert_fusion, bf16[512,1024]{1,0:T(8,128)(2,1)S(1)} %copy-done, s32[]{:T(128)S(6)} %select_n.16), kind=kOutput, calls=%fused_computation.9 | convolution fusion | flops 536870912 | bytes 3670020 | tf_op jit(solution)/shard_map/dot_general | solution.py:54
  55.6 0.0 collective-permute-done.1
  55.6 2.7 %multiply_reduce_fusion = (f32[]{:T(128)}, f32[512,1024]{1,0:T(8,128)S(1)}) fusion(f32[512,1024]{1,0:T(8,128)S(1)} %fusion.4, bf16[512,1024]{1,0:T(8,128)(2,1)} %collective-permute-done.1, bf16[512,1024]{1,0:T(8,128)(2,1)S(1)} %copy-done, s32[]{:T(128)S(6)} %select_n.17), kind=kOutput, calls=%fused_computation.1 | convolution fusion | flops 538443776 | bytes 5767176 | tf_op jit(solution)/shard_map/dot_general | solution.py:55
  58.3 1.4 %pad_maximum_fusion = f32[2]{0:T(128)S(1)} fusion(f32[1]{0:T(128)} %bitcast.3, f32[1]{0:T(128)} %bitcast.2), kind=kLoop, calls=%fused_computation.17 | loop fusion | flops 2 | bytes 16 | tf_op jit(solution)/shard_map/stack | solution.py:61
  59.7 4.0 %collective-permute-start.2 = (f32[2]{0:T(128)S(1)}, f32[2]{0:T(128)S(1)}, u32[]{:S(2)}, u32[]{:S(2)}) collective-permute-start(f32[2]{0:T(128)S(1)} %pad_maximum_fusion), channel_id=1, source_target_pairs={{0,1},{1,0},{2,3},{3,2},{4,5},{5,4},{6,7},{7,6},{8,9},{9,8},{10,11... | collective-permute-start | bytes 32 | tf_op jit(solution)/shard_map/ppermute | solution.py:22
  63.7 0.8 %collective-permute-done.2 = f32[2]{0:T(128)S(1)} collective-permute-done((f32[2]{0:T(128)S(1)}, f32[2]{0:T(128)S(1)}, u32[]{:S(2)}, u32[]{:S(2)}) %collective-permute-start.2) | collective-permute-done | bytes 40 | tf_op jit(solution)/shard_map/ppermute | solution.py:22
  64.5 0.7 fusion.10
  67.8 1.2 %multiply_convert_fusion = bf16[512,1024]{1,0:T(8,128)(2,1)} fusion(f32[512,1024]{1,0:T(8,128)S(1)} %get-tuple-element.8, f32[]{:T(128)S(6)} %mul.29), kind=kLoop, calls=%fused_computation | loop fusion | flops 1048576 | bytes 3145732 | tf_op jit(solution)/shard_map/convert_element_type | solution.py:70
Async XLA Ops:
  0.0 54.9 %copy-start = (bf16[512,1024]{1,0:T(8,128)(2,1)S(1)}, bf16[512,1024]{1,0:T(8,128)(2,1)}, u32[]{:S(2)}) copy-start(bf16[512,1024]{1,0:T(8,128)(2,1)} %param.4) | copy-start | bytes 3145732
  0.0 11.5 %copy-start.1 = (bf16[512,1024]{1,0:T(8,128)(2,1)S(1)}, bf16[512,1024]{1,0:T(8,128)(2,1)}, u32[]{:S(2)}) copy-start(bf16[512,1024]{1,0:T(8,128)(2,1)} %param.3) | copy-start | bytes 3145732
  0.0 11.5 %collective-permute-start = (bf16[512,1024]{1,0:T(8,128)(2,1)}, bf16[512,1024]{1,0:T(8,128)(2,1)}, u32[]{:S(2)}, u32[]{:S(2)}) collective-permute-start(bf16[512,1024]{1,0:T(8,128)(2,1)} %param.5), channel_id=1, source_target_pairs={{0,1},{1,0},{2,3},{3,2},{4,5},{5,4},{6,7},{7,6},{8,9},{9,8},{10,11... | collective-permute-start | bytes 3145736 | tf_op jit(solution)/shard_map/ppermute | solution.py:22
  13.4 42.2 %collective-permute-start.1 = (bf16[512,1024]{1,0:T(8,128)(2,1)S(1)}, bf16[512,1024]{1,0:T(8,128)(2,1)}, u32[]{:S(2)}, u32[]{:S(2)}) collective-permute-start(bf16[512,1024]{1,0:T(8,128)(2,1)S(1)} %add_convert_fusion), channel_id=1, source_target_pairs={{0,1},{1,0},{2,3},{3,2},{4,5},{5,4},{6,7},{7,6},{8,9},{9,8},{10,11... | collective-permute-start | bytes 3145736 | tf_op jit(solution)/shard_map/ppermute | solution.py:22
  59.7 4.8 %collective-permute-start.2 = (f32[2]{0:T(128)S(1)}, f32[2]{0:T(128)S(1)}, u32[]{:S(2)}, u32[]{:S(2)}) collective-permute-start(f32[2]{0:T(128)S(1)} %pad_maximum_fusion), channel_id=1, source_target_pairs={{0,1},{1,0},{2,3},{3,2},{4,5},{5,4},{6,7},{7,6},{8,9},{9,8},{10,11... | collective-permute-start | bytes 32 | tf_op jit(solution)/shard_map/ppermute | solution.py:22

commit v2 on v0

v2 whole, which is shorter than its diff:
```python
import functools

import jax
import jax.numpy as jnp
from jax import lax
from jax.experimental import pallas as pl
from jax.experimental.pallas import tpu as pltpu
from jax.sharding import Mesh
from jax.sharding import PartitionSpec as P

BLK = 1024
PLANE = ("row_1", "col_0", "col_1", "col_2")
LINE = "row_0"
PAIR = "col_2"
ALL = ("row_0", "row_1", "col_0", "col_1", "col_2")
EARLY_PLANES = 5
TILE = 256
LANES = 128

epsilon = 1e-06
clip_rms = 1.0
f32 = jnp.float32


def partner(shard, axis):
    return lax.ppermute(shard, axis, [(i, i ^ 1) for i in range(lax.axis_size(axis))])


def in_hbm(array):
    return pltpu.with_memory_space_constraint(array, pltpu.HBM)


def in_vmem(array):
    return pltpu.with_memory_space_constraint(array, pltpu.VMEM)


def squares(values):
    values = values.astype(f32)
    rows, columns = values.shape
    return jnp.sum((values * values).reshape(rows // 8, 8, columns), axis=0)


def lane_sums(partial):
    rows = jnp.sum(partial, axis=0, keepdims=True)
    return sum(rows[:, i : i + LANES] for i in range(0, rows.shape[1], LANES))


def head_kernel(grad, left, right, held, sent, sems):
    rows = grad.shape[0]
    step = rows // 4
    pieces = []
    for i in range(4):
        piece = pl.ds(i * step, step)
        pieces.append(
            pltpu.make_async_copy(grad.at[piece], held.at[0, piece], sems.at[i])
        )
    others = [
        pltpu.make_async_copy(right, held.at[1], sems.at[4]),
        pltpu.make_async_copy(left, held.at[2], sems.at[5]),
    ]
    for copy in pieces + others:
        copy.start()
    total = jnp.zeros((8, grad.shape[1]), f32)
    for i, copy in enumerate(pieces):
        copy.wait()
        total = total + squares(held[0, pl.ds(i * step, step), :])
    sent[...] = jnp.broadcast_to(lane_sums(total), sent.shape)
    for copy in others:
        copy.wait()


VMEM = pl.BlockSpec(memory_space=pltpu.VMEM)
HBM = pl.BlockSpec(memory_space=pltpu.HBM)


def head(grad, left, right, members):
    rows, columns = grad.shape
    return pl.pallas_call(
        head_kernel,
        out_shape=(
            pltpu.VMEM((3, rows, columns), grad.dtype),
            pltpu.VMEM((members, LANES), f32),
        ),
        in_specs=[HBM, HBM, HBM],
        out_specs=(VMEM, VMEM),
        scratch_shapes=[pltpu.SemaphoreType.DMA((6,))],
        cost_estimate=pl.CostEstimate(
            flops=2 * rows * columns, bytes_accessed=6 * rows * columns, transcendentals=0
        ),
        compiler_params=pltpu.CompilerParams(vmem_limit_bytes=16 << 20),
        name="head",
    )(grad, left, right)


def products(grad, left, right, heard, kept, ratio, own, theirs, applied, result, stats, sems):
    rows, columns = grad.shape
    tiles = columns // TILE
    sources = (grad, right, left)
    near_copies = [pltpu.make_async_copy(sources[i], own.at[i], sems.at[i]) for i in range(3)]
    far_copies = [pltpu.make_async_copy(heard.at[i], theirs.at[i], sems.at[3 + i]) for i in range(3)]
    for i in range(3):
        near_copies[i].start()
        far_copies[i].start()
    parity = lax.axis_index(PAIR)
    near = pl.ds(pl.multiple_of(parity * rows, rows), rows)
    far = pl.ds(pl.multiple_of((1 - parity) * rows, rows), rows)
    for i in range(2):
        near_copies[i].wait()
        far_copies[i].wait()

    def dot(a, b):
        return jnp.dot(a, b, preferred_element_type=f32)

    @pl.loop(0, tiles)
    def _(i):
        tile = pl.ds(pl.multiple_of(i * TILE, TILE), TILE)
        top, bottom = own[1, :, tile], theirs[1, :, tile]
        mine = dot(own[0, :, near], top) + dot(own[0, :, far], bottom)
        applied[0, :, tile] = mine.astype(jnp.bfloat16)
        yours = dot(theirs[0, :, near], top) + dot(theirs[0, :, far], bottom)
        applied[1, :, tile] = yours.astype(jnp.bfloat16)

    near_copies[2].wait()
    far_copies[2].wait()

    def write(i):
        tile = pl.ds(pl.multiple_of(i * TILE, TILE), TILE)
        return pltpu.make_async_copy(result.at[:, tile], kept.at[:, tile], sems.at[6 + i])

    def second(i, cond_sq):
        tile = pl.ds(pl.multiple_of(i * TILE, TILE), TILE)
        top, bottom = applied[0, :, tile], applied[1, :, tile]
        mine = dot(own[2, :, near], top) + dot(own[2, :, far], bottom)
        result[:, tile] = mine
        yours = dot(theirs[2, :, near], top) + dot(theirs[2, :, far], bottom)
        return cond_sq + squares(mine) + squares(yours)

    cond_sq = lax.fori_loop(0, tiles, second, jnp.zeros((8, TILE), f32))
    for i in range(tiles):
        write(i).start()
    grad_sq = squares(own[0]) + squares(theirs[0])
    entries = BLK * BLK
    grad_sq = jnp.sum(lane_sums(grad_sq), axis=1, keepdims=True)
    cond_sq = jnp.sum(lane_sums(cond_sq), axis=1, keepdims=True)
    stats[...] = jnp.broadcast_to(
        jnp.sqrt((grad_sq / entries + epsilon) / (cond_sq / entries + epsilon)), stats.shape
    )
    copy = pltpu.make_async_copy(stats, ratio, sems.at[6 + tiles])
    copy.start()
    for i in range(tiles):
        write(i).wait()
    copy.wait()


def middle_kernel(plane, grad, left, right, heard, sent, kept, ratio, *scratch):
    sent[...] = jnp.broadcast_to(jnp.sum(plane[...], axis=0, keepdims=True), sent.shape)

    @pl.when(lax.axis_index(LINE) < EARLY_PLANES)
    def _():
        products(grad, left, right, heard, kept, ratio, *scratch)


def late_kernel(grad, left, right, heard, kept_in, ratio_in, kept, ratio, *scratch):
    @pl.when(lax.axis_index(LINE) >= EARLY_PLANES)
    def _():
        products(grad, left, right, heard, kept, ratio, *scratch)


def work_scratch(rows, columns):
    return [
        pltpu.VMEM((3, rows, columns), jnp.bfloat16),
        pltpu.VMEM((3, rows, columns), jnp.bfloat16),
        pltpu.VMEM((2, rows, columns), jnp.bfloat16),
        pltpu.VMEM((rows, columns), f32),
        pltpu.VMEM((8, LANES), f32),
        pltpu.SemaphoreType.DMA((7 + columns // TILE,)),
    ]


def middle(plane, grad, left, right, heard, members):
    rows, columns = grad.shape
    return pl.pallas_call(
        middle_kernel,
        out_shape=(
            jax.ShapeDtypeStruct((members, LANES), f32),
            pltpu.HBM((rows, columns), f32),
            pltpu.HBM((8, LANES), f32),
        ),
        in_specs=[VMEM, HBM, HBM, HBM, HBM],
        out_specs=(VMEM, HBM, HBM),
        scratch_shapes=work_scratch(rows, columns),
        cost_estimate=pl.CostEstimate(flops=10**9, bytes_accessed=10**7, transcendentals=0),
        compiler_params=pltpu.CompilerParams(vmem_limit_bytes=32 << 20),
        name="middle",
    )(plane, grad, left, right, heard)


def late(grad, left, right, heard, kept, ratio):
    rows, columns = grad.shape
    return pl.pallas_call(
        late_kernel,
        out_shape=(
            jax.ShapeDtypeStruct(kept.shape, f32),
            jax.ShapeDtypeStruct(ratio.shape, f32),
        ),
        in_specs=[HBM] * 6,
        out_specs=(HBM, HBM),
        input_output_aliases={4: 0, 5: 1},
        scratch_shapes=work_scratch(rows, columns),
        cost_estimate=pl.CostEstimate(flops=4 * 10**9, bytes_accessed=10**7, transcendentals=0),
        name="late",
    )(grad, left, right, heard, kept, ratio)


def final_kernel(count, line, kept, ratio, update, taken, staged, stats, sems):
    step = kept.shape[0] // 4
    pieces = [pl.ds(i * step, step) for i in range(4)]
    stat_copy = pltpu.make_async_copy(ratio, stats, sems.at[8])
    stat_copy.start()
    reads = [
        pltpu.make_async_copy(kept.at[piece], taken.at[piece], sems.at[i])
        for i, piece in enumerate(pieces)
    ]
    for copy in reads:
        copy.start()
    total = jnp.sum(jnp.sum(line[...], axis=0, keepdims=True), axis=1, keepdims=True)
    clip = clip_rms / jnp.sqrt(total / count + epsilon)
    stat_copy.wait()
    scale = clip * stats[0:1, 0:1]
    writes = []
    for i, piece in enumerate(pieces):
        reads[i].wait()
        staged[piece, :] = (scale * taken[piece, :]).astype(jnp.bfloat16)
        writes.append(pltpu.make_async_copy(staged.at[piece], update.at[piece], sems.at[4 + i]))
        writes[-1].start()
    for copy in writes:
        copy.wait()


def final(line, kept, ratio, count):
    rows, columns = kept.shape
    return pl.pallas_call(
        functools.partial(final_kernel, count),
        out_shape=jax.ShapeDtypeStruct((rows, columns), jnp.bfloat16),
        in_specs=[VMEM, HBM, HBM],
        out_specs=HBM,
        scratch_shapes=[
            pltpu.VMEM((rows, columns), f32),
            pltpu.VMEM((rows, columns), jnp.bfloat16),
            pltpu.VMEM((8, LANES), f32),
            pltpu.SemaphoreType.DMA((9,)),
        ],
        compiler_params=pltpu.CompilerParams(vmem_limit_bytes=16 << 20),
        name="final",
    )(line, kept, ratio)


def shards(grad, left_root, right_root):
    plane_size, line_size = lax.axis_size(PLANE), lax.axis_size(LINE)
    count = float(plane_size * line_size // 2 * BLK * BLK)
    grad, left_root, right_root = (in_hbm(x) for x in (grad, left_root, right_root))
    held, sent = head(grad, left_root, right_root, plane_size)
    with jax.named_scope("plane"):
        plane = lax.all_to_all(sent, PLANE, 0, 0, tiled=True)
    with jax.named_scope("exchange"):
        heard = in_hbm(partner(held, PAIR))
    sent, kept, ratio = middle(in_vmem(plane), grad, left_root, right_root, heard, line_size)
    with jax.named_scope("line"):
        line = lax.all_to_all(sent, LINE, 0, 0, tiled=True)
    kept, ratio = late(grad, left_root, right_root, heard, kept, ratio)
    return final(in_vmem(line), in_hbm(kept), in_hbm(ratio), count)


def solution(mesh):
    torus = Mesh(mesh.devices.reshape(16, 2, 4, 2, 2), ALL)
    return jax.shard_map(
        shards,
        mesh=torus,
        in_specs=(P(ALL, None), P(ALL, None), P(ALL, None)),
        out_specs=P(ALL, None),
        check_vma=False,
    )
```

time: 89.1 us -> 53 us (0.59)
  blocking collectives: 58.6 us -> 9.62 us
  Pallas kernels: 0 us -> 14.3 us
  waiting for transfers between devices: 1.27 us -> 11.1 us
  matrix products: 7.48 us -> 0 us
  other arithmetic: 3.84 us -> 0 us
  between operations: 3.46 us -> 0.04 us
  starting transfers between devices: 13.4 us -> 16 us
  local copies, waits for them, and re-layouts: 0.67 us -> 1.65 us
    psum x5 -> x0, blocking collectives: 58.6 us -> none  [over_axes(): return functools.reduce(lax.psum, axes, shard)]
    pallas_call x0 -> x4, Pallas kernels: none -> 14.3 us  [the longest x1 9.98 us: middle(): pl.pallas_call(middle_kernel, out_shape=(jax.ShapeDtypeStruct((members, L...]
    all_to_all x0 -> x1, waiting for transfers between devices: none -> 11.1 us  [shards(): line = lax.all_to_all(sent, LINE, 0, 0, tiled=True)]
    all_to_all x0 -> x1, blocking collectives: none -> 9.62 us  [shards(): plane = lax.all_to_all(sent, PLANE, 0, 0, tiled=True)]
    dot_general x4 -> x0, matrix products: 7.48 us -> none  [the longest x1 2.7 us: shards(): jnp.dot(other_left, partner_rows, preferred_element_type=jnp.float32)]
    all_to_all x0 -> x1, starting transfers between devices: none -> 7.26 us  [shards(): line = lax.all_to_all(sent, LINE, 0, 0, tiled=True)]
    ppermute x3 -> x1, starting transfers between devices: 13.4 us -> 8.75 us  [partner(): lax.ppermute(shard, axis, [(i, i ^ 1) for i in range(lax.axis_size(axis))])]
    unnamed x4 -> x2, local copies, waits for them, and re-layouts: 0.01 us -> 1.65 us
  transfers between devices with their start and end apart: 3 -> 2, of which waited for: 2 -> 1; matrix products, arithmetic and copies ran while one was open for 5% -> 0% of each run, Pallas kernels for 0% -> 0%
where the time goes in v2:
time: 53 us; the launch traced here: 52.8 us
  starting transfers between devices  16 us (30%)
  Pallas kernels  14.3 us (27%)
  waiting for transfers between devices  11.1 us (21%)
  blocking collectives  9.62 us (18%)
  local copies, waits for them, and re-layouts  1.65 us (3%)
    all_to_all x1, waiting for transfers between devices, shards(): line = lax.all_to_all(sent, LINE, 0, 0, tiled=True)  11.1 us
    pallas_call x1, Pallas kernels, middle(): pl.pallas_call(middle_kernel, out_shape=(jax.ShapeDtypeStruct((members, L...  9.98 us
    all_to_all x1, blocking collectives, shards(): plane = lax.all_to_all(sent, PLANE, 0, 0, tiled=True)  9.62 us
    ppermute x1, starting transfers between devices, partner(): lax.ppermute(shard, axis, [(i, i ^ 1) for i in range(lax.axis_size(axis))])  8.75 us
    all_to_all x1, starting transfers between devices, shards(): line = lax.all_to_all(sent, LINE, 0, 0, tiled=True)  7.26 us
    pallas_call x1, Pallas kernels, final(): pl.pallas_call(functools.partial(final_kernel, count), out_shape=jax.Shap...  2.33 us
    pallas_call x1, Pallas kernels, head(): pl.pallas_call(head_kernel, out_shape=(pltpu.VMEM((3, rows, columns), gra...  1.92 us
    unnamed x2, local copies, waits for them, and re-layouts  1.65 us
  transfers between devices with their start and end apart: 2, of which 1 were waited for; matrix products, arithmetic and copies ran while one was open for 0% of the time, Pallas kernels for 0%

profile of v2, /device:TPU:1, one launch (start us, length us, event | category | flops | bytes accessed | tf_op | source)
XLA Modules:
  0.0 52.8 jit_solution(14563967554608311579)
XLA Ops:
  0.0 1.9 %head.1 = (bf16[3,512,1024]{2,1,0:T(8,128)(2,1)S(1)}, f32[32,128]{1,0:T(8,128)S(1)}) custom-call(bf16[512,1024]{1,0:T(8,128)(2,1)} %grad.5, bf16[512,1024]{1,0:T(8,128)(2,1)} %left.5, bf16[512,1024]{1,0:T(8,128)(2,1)} %right.5), custom_call_target="tpu_custom_call" | custom-call | flops 1048576 | bytes 3145728 | tf_op jit(solution)/shard_map/head/pallas_call | solution.py:78
  1.9 8.7 %collective-permute-start = (bf16[3,512,1024]{2,1,0:T(8,128)(2,1)S(1)}, bf16[3,512,1024]{2,1,0:T(8,128)(2,1)S(1)}, u32[]{:S(2)}, u32[]{:S(2)}) collective-permute-start(bf16[3,512,1024]{2,1,0:T(8,128)(2,1)S(1)} %get-tuple-element.13), channel_id=1, source_target_pairs={{0,1},{1,0},{2,3},{3,2},{4,5},{5,4},{6,7},{7,6},{8,9},{9,8},{10,11... | collective-permute-start | bytes 9437192 | tf_op jit(solution)/shard_map/exchange/ppermute | solution.py:26
  10.7 9.6 %all_to_all.22 = f32[32,1,128]{2,1,0:T(1,128)S(1)} all-to-all(f32[32,1,128]{2,1,0:T(1,128)S(1)} %bitcast.10), channel_id=1, replica_groups=mesh['row_0'=16,'row_1'=2,'col_0'=4,'col_1'=2,'col_2'=2] {'row_1','col_0..., dimensions={0} | all-to-all | bytes 32768 | tf_op jit(solution)/shard_map/plane/all_to_all | solution.py:264
  20.3 0.0 collective-permute-done.heard
  20.3 0.0 copy-start
  20.3 1.6 %copy-done = bf16[3,512,1024]{2,1,0:T(8,128)(2,1)} copy-done((bf16[3,512,1024]{2,1,0:T(8,128)(2,1)}, bf16[3,512,1024]{2,1,0:T(8,128)(2,1)S(1)}, u32[]{:S(2)}) %copy-start) | copy-done | bytes 3145752
  22.0 10.0 %middle.1 = (f32[16,128]{1,0:T(8,128)}, f32[512,1024]{1,0:T(8,128)}, f32[8,128]{1,0:T(8,128)}) custom-call(f32[32,128]{1,0:T(8,128)S(1)} %bitcast.8, bf16[512,1024]{1,0:T(8,128)(2,1)} %grad.5, bf16[512,1024]{1,0:T(8,128)(2,1)} %left.5, bf16[512,1024]{1,0:T(8,128)(2,1)} %right.5, bf16[3,512,1024]{2,1,0:T(8,128)(2,1)} %copy-done), custom_call_target="tpu_custom_call" | custom-call | flops 1000000000 | bytes 10000000 | tf_op jit(solution)/shard_map/middle/pallas_call | solution.py:182
  31.9 7.3 %all-to-all-start.1 = ((f32[16,1,128]{2,1,0:T(1,128)}), f32[16,1,128]{2,1,0:T(1,128)S(1)}, u32[]{:S(2)}, u32[]{:S(2)}) async-start(f32[16,1,128]{2,1,0:T(1,128)} %bitcast.4), calls=%async_computation.1 | async-start | bytes 16384 | tf_op jit(solution)/shard_map/line/all_to_all | solution.py:269
  39.2 0.1 late.1
  39.3 11.1 %all-to-all-done.1 = f32[16,1,128]{2,1,0:T(1,128)S(1)} async-done(((f32[16,1,128]{2,1,0:T(1,128)}), f32[16,1,128]{2,1,0:T(1,128)S(1)}, u32[]{:S(2)}, u32[]{:S(2)}) %all-to-all-start.1) | async-done | bytes 8224 | tf_op jit(solution)/shard_map/line/all_to_all | solution.py:269
  50.5 2.3 %final.1 = bf16[512,1024]{1,0:T(8,128)(2,1)} custom-call(f32[16,128]{1,0:T(8,128)S(1)} %bitcast.9, f32[512,1024]{1,0:T(8,128)} %get-tuple-element.17.kept, f32[8,128]{1,0:T(8,128)} %get-tuple-element.18.ratio), custom_call_target="tpu_custom_call" | custom-call | tf_op jit(solution)/shard_map/final/pallas_call | solution.py:242
Async XLA Ops:
  1.9 18.4 %collective-permute-start = (bf16[3,512,1024]{2,1,0:T(8,128)(2,1)S(1)}, bf16[3,512,1024]{2,1,0:T(8,128)(2,1)S(1)}, u32[]{:S(2)}, u32[]{:S(2)}) collective-permute-start(bf16[3,512,1024]{2,1,0:T(8,128)(2,1)S(1)} %get-tuple-element.13), channel_id=1, source_target_pairs={{0,1},{1,0},{2,3},{3,2},{4,5},{5,4},{6,7},{7,6},{8,9},{9,8},{10,11... | collective-permute-start | bytes 9437192 | tf_op jit(solution)/shard_map/exchange/ppermute | solution.py:26
  20.3 1.7 %copy-start = (bf16[3,512,1024]{2,1,0:T(8,128)(2,1)}, bf16[3,512,1024]{2,1,0:T(8,128)(2,1)S(1)}, u32[]{:S(2)}) copy-start(bf16[3,512,1024]{2,1,0:T(8,128)(2,1)S(1)} %collective-permute-done.heard) | copy-start | bytes 9437188
  31.9 18.5 %all-to-all-start.1 = ((f32[16,1,128]{2,1,0:T(1,128)}), f32[16,1,128]{2,1,0:T(1,128)S(1)}, u32[]{:S(2)}, u32[]{:S(2)}) async-start(f32[16,1,128]{2,1,0:T(1,128)} %bitcast.4), calls=%async_computation.1 | async-start | bytes 16384 | tf_op jit(solution)/shard_map/line/all_to_all | solution.py:269

commit v3 on v2

v3 whole, which is shorter than its diff:
```python
import functools

import jax
import jax.numpy as jnp
from jax import lax
from jax.experimental import pallas as pl
from jax.experimental.pallas import tpu as pltpu
from jax.sharding import Mesh
from jax.sharding import PartitionSpec as P

BLK = 1024
LINE, PLANE = "line", "plane"
ALL = (LINE, PLANE)
LINE_FIRST = 10
PLANE_FIRST = 30
EARLY_PLANES = 4
LANES = 128

epsilon = 1e-06
clip_rms = 1.0
f32 = jnp.float32


def partner(shard, axis):
    return lax.ppermute(shard, axis, [(i, i ^ 1) for i in range(lax.axis_size(axis))])


def tell_all(rows, axis, first):
    members = lax.axis_size(axis)
    group = [(first + i) % members for i in range(members)]
    return lax.all_to_all(rows, axis, 0, 0, axis_index_groups=[group], tiled=True)


def in_hbm(array):
    return pltpu.with_memory_space_constraint(array, pltpu.HBM)


def in_vmem(array):
    return pltpu.with_memory_space_constraint(array, pltpu.VMEM)


def squares(values):
    values = values.astype(f32)
    rows, columns = values.shape
    return jnp.sum((values * values).reshape(rows // 8, 8, columns), axis=0)


def lane_sums(partial):
    rows = jnp.sum(partial, axis=0, keepdims=True)
    return sum(rows[:, i : i + LANES] for i in range(0, rows.shape[1], LANES))


def head_kernel(grad, left, right, held, sent, sems):
    rows = grad.shape[0]
    step = rows // 4
    pieces = []
    for i in range(4):
        piece = pl.ds(i * step, step)
        pieces.append(
            pltpu.make_async_copy(grad.at[piece], held.at[0, piece], sems.at[i])
        )
    others = [
        pltpu.make_async_copy(right, held.at[1], sems.at[4]),
        pltpu.make_async_copy(left, held.at[2], sems.at[5]),
    ]
    for copy in pieces + others:
        copy.start()
    total = jnp.zeros((8, grad.shape[1]), f32)
    for i, copy in enumerate(pieces):
        copy.wait()
        total = total + squares(held[0, pl.ds(i * step, step), :])
    sent[...] = jnp.broadcast_to(lane_sums(total), sent.shape)
    for copy in others:
        copy.wait()


VMEM = pl.BlockSpec(memory_space=pltpu.VMEM)
HBM = pl.BlockSpec(memory_space=pltpu.HBM)
ANY = pl.BlockSpec(memory_space=pl.ANY)


def head(grad, left, right, members):
    rows, columns = grad.shape
    return pl.pallas_call(
        head_kernel,
        out_shape=(
            pltpu.VMEM((3, rows, columns), grad.dtype),
            pltpu.VMEM((members, LANES), f32),
        ),
        in_specs=[HBM, HBM, HBM],
        out_specs=(VMEM, VMEM),
        scratch_shapes=[pltpu.SemaphoreType.DMA((6,))],
        cost_estimate=pl.CostEstimate(
            flops=2 * rows * columns, bytes_accessed=6 * rows * columns, transcendentals=0
        ),
        compiler_params=pltpu.CompilerParams(vmem_limit_bytes=16 << 20),
        name="head",
    )(grad, left, right)


def products(own, held, ratio, applied, ready):
    rows = own.shape[1]
    parity = lax.axis_index(PLANE) % 2
    near = pl.ds(pl.multiple_of(parity * rows, rows), rows)
    far = pl.ds(pl.multiple_of((1 - parity) * rows, rows), rows)

    def both(left, top, bottom):
        first = jnp.dot(left[:, near], top[...], preferred_element_type=f32)
        return first + jnp.dot(left[:, far], bottom[...], preferred_element_type=f32)

    ready(1)
    applied[1] = both(held.at[0], own.at[1], held.at[1]).astype(jnp.bfloat16)
    grad_sq = squares(held[0])
    ready(0)
    applied[0] = both(own.at[0], own.at[1], held.at[1]).astype(jnp.bfloat16)
    grad_sq = grad_sq + squares(own[0])
    ready(2)
    result = both(own.at[2], applied.at[0], applied.at[1])
    upper = result.astype(jnp.bfloat16)
    held[0] = upper
    held[1] = (result - upper.astype(f32)).astype(jnp.bfloat16)
    cond_sq = squares(result) + squares(both(held.at[2], applied.at[0], applied.at[1]))
    entries = BLK * BLK
    grad_sq = jnp.sum(lane_sums(grad_sq), axis=1, keepdims=True)
    cond_sq = jnp.sum(lane_sums(cond_sq), axis=1, keepdims=True)
    ratio[...] = jnp.broadcast_to(
        jnp.sqrt((grad_sq / entries + epsilon) / (cond_sq / entries + epsilon)), ratio.shape
    )


def middle_kernel(plane, own, heard, sent, held, ratio, applied):
    sent[...] = jnp.broadcast_to(jnp.sum(plane[...], axis=0, keepdims=True), sent.shape)

    @pl.when(lax.axis_index(LINE) < EARLY_PLANES)
    def _():
        products(own, held, ratio, applied, lambda i: None)


def late_kernel(grad, right, left, heard, held, ratio, applied, own, sems):
    @pl.when(lax.axis_index(LINE) >= EARLY_PLANES)
    def _():
        copies = [
            pltpu.make_async_copy(source, own.at[i], sems.at[i])
            for i, source in enumerate((grad, right, left))
        ]
        for i in (1, 0, 2):
            copies[i].start()
        products(own, held, ratio, applied, lambda i: copies[i].wait())


def middle(plane, own, heard, members):
    _, rows, columns = heard.shape
    return pl.pallas_call(
        middle_kernel,
        out_shape=(
            pltpu.VMEM((members, LANES), f32),
            pltpu.VMEM(heard.shape, heard.dtype),
            pltpu.VMEM((8, LANES), f32),
        ),
        in_specs=[VMEM] * 3,
        out_specs=(VMEM,) * 3,
        input_output_aliases={2: 1},
        scratch_shapes=[pltpu.VMEM((2, rows, columns), jnp.bfloat16)],
        compiler_params=pltpu.CompilerParams(vmem_limit_bytes=24 << 20),
        cost_estimate=pl.CostEstimate(flops=10**9, bytes_accessed=10**7, transcendentals=0),
        name="middle",
    )(plane, own, heard)


def late(grad, right, left, heard):
    _, rows, columns = heard.shape
    return pl.pallas_call(
        late_kernel,
        out_shape=(pltpu.VMEM(heard.shape, heard.dtype), pltpu.VMEM((8, LANES), f32)),
        in_specs=[HBM, HBM, HBM, VMEM],
        out_specs=(VMEM, VMEM),
        input_output_aliases={3: 0},
        scratch_shapes=[
            pltpu.VMEM((2, rows, columns), jnp.bfloat16),
            pltpu.VMEM(heard.shape, heard.dtype),
            pltpu.SemaphoreType.DMA((3,)),
        ],
        compiler_params=pltpu.CompilerParams(vmem_limit_bytes=24 << 20),
        cost_estimate=pl.CostEstimate(flops=4 * 10**9, bytes_accessed=10**7, transcendentals=0),
        name="late",
    )(grad, right, left, heard)


def final_kernel(count, line, held, early_ratio, late_ratio, update, staged, sems):
    rows = held.shape[1]
    step = rows // 4
    total = jnp.sum(jnp.sum(line[...], axis=0, keepdims=True), axis=1, keepdims=True)
    clip = clip_rms / jnp.sqrt(total / count + epsilon)
    early = lax.axis_index(LINE) < EARLY_PLANES
    scale = clip * jnp.where(early, early_ratio[0:1, 0:1], late_ratio[0:1, 0:1])
    writes = []
    for i in range(4):
        piece = pl.ds(i * step, step)
        result = held[0, piece, :].astype(f32) + held[1, piece, :].astype(f32)
        staged[piece, :] = (scale * result).astype(jnp.bfloat16)
        writes.append(pltpu.make_async_copy(staged.at[piece], update.at[piece], sems.at[i]))
        writes[-1].start()
    for copy in writes:
        copy.wait()


def final(count, line, held, early_ratio, late_ratio):
    _, rows, columns = held.shape
    return pl.pallas_call(
        functools.partial(final_kernel, count),
        out_shape=jax.ShapeDtypeStruct((rows, columns), jnp.bfloat16),
        in_specs=[VMEM] * 4,
        out_specs=HBM,
        scratch_shapes=[
            pltpu.VMEM((rows, columns), jnp.bfloat16),
            pltpu.SemaphoreType.DMA((4,)),
        ],
        compiler_params=pltpu.CompilerParams(vmem_limit_bytes=16 << 20),
        name="final",
    )(line, held, early_ratio, late_ratio)


def shards(grad, left_root, right_root):
    plane_size, line_size = lax.axis_size(PLANE), lax.axis_size(LINE)
    count = float(plane_size * line_size // 2 * BLK * BLK)
    grad, left_root, right_root = (in_hbm(x) for x in (grad, left_root, right_root))
    own, sent = head(grad, left_root, right_root, plane_size)
    with jax.named_scope("plane"):
        plane = tell_all(sent, PLANE, PLANE_FIRST)
    with jax.named_scope("exchange"):
        heard = partner(own, PLANE)
    sent, held, early_ratio = middle(in_vmem(plane), own, heard, line_size)
    with jax.named_scope("line"):
        line = tell_all(sent, LINE, LINE_FIRST)
    held, late_ratio = late(grad, right_root, left_root, held)
    return final(count, in_vmem(line), held, early_ratio, late_ratio)


def solution(mesh):
    torus = Mesh(mesh.devices.reshape(16, 32), ALL)
    return jax.shard_map(
        shards,
        mesh=torus,
        in_specs=(P(ALL, None), P(ALL, None), P(ALL, None)),
        out_specs=P(ALL, None),
        check_vma=False,
    )
```

time: 53 us -> 40.7 us (0.77)
  waiting for transfers between devices: 11.1 us -> 3.26 us
  Pallas kernels: 14.3 us -> 8.71 us
  starting transfers between devices: 16 us -> 18.4 us
  local copies, waits for them, and re-layouts: 1.65 us -> 0 us
    all_to_all x1, waiting for transfers between devices: 11.1 us -> 3.26 us  [tell_all(): lax.all_to_all(rows, axis, 0, 0, axis_index_groups=[group], tiled=True)]
    pallas_call x2, Pallas kernels: 10.1 us -> 5.51 us  [the longest x1 5.48 us: middle(): pl.pallas_call(middle_kernel, out_shape=(pltpu.VMEM((members, LANES), f32...]
    all_to_all x1, starting transfers between devices: 7.26 us -> 9.67 us  [tell_all(): lax.all_to_all(rows, axis, 0, 0, axis_index_groups=[group], tiled=True)]
    unnamed x2 -> x0, local copies, waits for them, and re-layouts: 1.65 us -> none
    pallas_call x1, Pallas kernels: 2.33 us -> 1.28 us  [final(): pl.pallas_call(functools.partial(final_kernel, count), out_shape=jax.Shap...]
where the time goes in v3:
time: 40.7 us; the launch traced here: 40.5 us
  starting transfers between devices  18.4 us (45%)
  blocking collectives  10.1 us (25%)
  Pallas kernels  8.71 us (21%)
  waiting for transfers between devices  3.26 us (8%)
    all_to_all x1, blocking collectives, tell_all(): lax.all_to_all(rows, axis, 0, 0, axis_index_groups=[group], tiled=True)  10.1 us
    all_to_all x1, starting transfers between devices, tell_all(): lax.all_to_all(rows, axis, 0, 0, axis_index_groups=[group], tiled=True)  9.67 us
    ppermute x1, starting transfers between devices, partner(): lax.ppermute(shard, axis, [(i, i ^ 1) for i in range(lax.axis_size(axis))])  8.75 us
    pallas_call x1, Pallas kernels, middle(): pl.pallas_call(middle_kernel, out_shape=(pltpu.VMEM((members, LANES), f32...  5.48 us
    all_to_all x1, waiting for transfers between devices, tell_all(): lax.all_to_all(rows, axis, 0, 0, axis_index_groups=[group], tiled=True)  3.26 us
    pallas_call x1, Pallas kernels, head(): pl.pallas_call(head_kernel, out_shape=(pltpu.VMEM((3, rows, columns), gra...  1.92 us
    pallas_call x1, Pallas kernels, final(): pl.pallas_call(functools.partial(final_kernel, count), out_shape=jax.Shap...  1.28 us
  transfers between devices with their start and end apart: 2, of which 1 were waited for; matrix products, arithmetic and copies ran while one was open for 0% of the time, Pallas kernels for 0%

profile of v3, /device:TPU:1, one launch (start us, length us, event | category | flops | bytes accessed | tf_op | source)
XLA Modules:
  0.0 40.5 jit_solution(4261020865154116577)
XLA Ops:
  0.0 1.9 %head.1 = (bf16[3,512,1024]{2,1,0:T(8,128)(2,1)S(1)}, f32[32,128]{1,0:T(8,128)S(1)}) custom-call(bf16[512,1024]{1,0:T(8,128)(2,1)} %grad.3, bf16[512,1024]{1,0:T(8,128)(2,1)} %left.3, bf16[512,1024]{1,0:T(8,128)(2,1)} %right.3), custom_call_target="tpu_custom_call" | custom-call | flops 1048576 | bytes 3145728 | tf_op jit(solution)/shard_map/head/pallas_call | solution.py:84
  1.9 8.7 %collective-permute-start = (bf16[3,512,1024]{2,1,0:T(8,128)(2,1)S(1)}, bf16[3,512,1024]{2,1,0:T(8,128)(2,1)S(1)}, u32[]{:S(2)}, u32[]{:S(2)}) collective-permute-start(bf16[3,512,1024]{2,1,0:T(8,128)(2,1)S(1)} %get-tuple-element.13.own), channel_id=1, source_target_pairs={{0,1},{1,0},{2,3},{3,2},{4,5},{5,4},{6,7},{7,6},{8,9},{9,8},{10,11... | collective-permute-start | bytes 9437192 | tf_op jit(solution)/shard_map/exchange/ppermute | solution.py:25
  10.7 10.1 %all_to_all.22 = f32[32,1,128]{2,1,0:T(1,128)S(1)} all-to-all(f32[32,1,128]{2,1,0:T(1,128)S(1)} %bitcast.10), channel_id=1, replica_groups={{30,31,0,1,2,3,4,5,6,7,8,9,10,11,12,13,14,15,16,17,18,19,20,21,22,23,24..., dimensions={0} | all-to-all | bytes 32768 | tf_op jit(solution)/shard_map/plane/all_to_all | solution.py:31
  20.7 0.0 collective-permute-done.heard
  20.7 5.5 %middle.1 = (f32[16,128]{1,0:T(8,128)}, bf16[3,512,1024]{2,1,0:T(8,128)(2,1)S(1)}, f32[8,128]{1,0:T(8,128)S(1)}) custom-call(f32[32,128]{1,0:T(8,128)S(1)} %bitcast.8, bf16[3,512,1024]{2,1,0:T(8,128)(2,1)S(1)} %get-tuple-element.13.own, bf16[3,512,1024]{2,1,0:T(8,128)(2,1)S(1)} %collective-permute-done.heard), custom_call_target="tpu_custom_call", output_to_operand_aliasing={{1}: (2, {})} | custom-call | flops 1000000000 | bytes 10000000 | tf_op jit(solution)/shard_map/middle/pallas_call | solution.py:153
  26.2 9.7 %all-to-all-start.1 = ((f32[16,1,128]{2,1,0:T(1,128)}), f32[16,1,128]{2,1,0:T(1,128)S(1)}, u32[]{:S(2)}, u32[]{:S(2)}) async-start(f32[16,1,128]{2,1,0:T(1,128)} %bitcast.4), calls=%async_computation.1 | async-start | bytes 16384 | tf_op jit(solution)/shard_map/line/all_to_all | solution.py:31
  35.9 3.3 %all-to-all-done.1 = f32[16,1,128]{2,1,0:T(1,128)S(1)} async-done(((f32[16,1,128]{2,1,0:T(1,128)}), f32[16,1,128]{2,1,0:T(1,128)S(1)}, u32[]{:S(2)}, u32[]{:S(2)}) %all-to-all-start.1) | async-done | bytes 8224 | tf_op jit(solution)/shard_map/line/all_to_all | solution.py:31
  39.2 1.3 %final.1 = bf16[512,1024]{1,0:T(8,128)(2,1)} custom-call(f32[16,128]{1,0:T(8,128)S(1)} %bitcast.9, bf16[3,512,1024]{2,1,0:T(8,128)(2,1)S(1)} %get-tuple-element.16.held, f32[8,128]{1,0:T(8,128)S(1)} %get-tuple-element.17.early_ratio, f32[8,128]{1,0:T(8,128)S(1)} %get-tuple-element.18.late_ratio), custom_call_target="tpu_custom_call" | custom-call | tf_op jit(solution)/shard_map/final/pallas_call | solution.py:209
  (1 shorter events, 0.0 us)
Async XLA Ops:
  1.9 18.8 %collective-permute-start = (bf16[3,512,1024]{2,1,0:T(8,128)(2,1)S(1)}, bf16[3,512,1024]{2,1,0:T(8,128)(2,1)S(1)}, u32[]{:S(2)}, u32[]{:S(2)}) collective-permute-start(bf16[3,512,1024]{2,1,0:T(8,128)(2,1)S(1)} %get-tuple-element.13.own), channel_id=1, source_target_pairs={{0,1},{1,0},{2,3},{3,2},{4,5},{5,4},{6,7},{7,6},{8,9},{9,8},{10,11... | collective-permute-start | bytes 9437192 | tf_op jit(solution)/shard_map/exchange/ppermute | solution.py:25
  26.2 13.0 %all-to-all-start.1 = ((f32[16,1,128]{2,1,0:T(1,128)}), f32[16,1,128]{2,1,0:T(1,128)S(1)}, u32[]{:S(2)}, u32[]{:S(2)}) async-start(f32[16,1,128]{2,1,0:T(1,128)} %bitcast.4), calls=%async_computation.1 | async-start | bytes 16384 | tf_op jit(solution)/shard_map/line/all_to_all | solution.py:31

commit v4 on v3

--- a/solution.py
+++ b/solution.py
@@ -12,7 +12,7 @@
 LINE, PLANE = "line", "plane"
 ALL = (LINE, PLANE)
 LINE_FIRST = 10
-PLANE_FIRST = 30
+PLANE_FIRST = 11
 EARLY_PLANES = 4
 LANES = 128
 
@@ -98,101 +98,124 @@
     )(grad, left, right)
 
 
-def products(own, held, ratio, applied, ready):
-    rows = own.shape[1]
+def sides(rows):
     parity = lax.axis_index(PLANE) % 2
     near = pl.ds(pl.multiple_of(parity * rows, rows), rows)
     far = pl.ds(pl.multiple_of((1 - parity) * rows, rows), rows)
-
-    def both(left, top, bottom):
-        first = jnp.dot(left[:, near], top[...], preferred_element_type=f32)
-        return first + jnp.dot(left[:, far], bottom[...], preferred_element_type=f32)
-
+    return near, far
+
+
+def dot(a, b):
+    return jnp.dot(a, b, preferred_element_type=f32)
+
+
+def total(partial):
+    return jnp.sum(lane_sums(partial), axis=1, keepdims=True)
+
+
+def first_half(grad, right, held, grad_sq, ready):
+    near, far = sides(grad.shape[0])
+    ready(0)
+    yours = dot(held[0, :, near], right[...]) + dot(held[0, :, far], held[1])
+    squared = squares(held[0])
+    held[0] = yours.astype(jnp.bfloat16)
     ready(1)
-    applied[1] = both(held.at[0], own.at[1], held.at[1]).astype(jnp.bfloat16)
-    grad_sq = squares(held[0])
-    ready(0)
-    applied[0] = both(own.at[0], own.at[1], held.at[1]).astype(jnp.bfloat16)
-    grad_sq = grad_sq + squares(own[0])
-    ready(2)
-    result = both(own.at[2], applied.at[0], applied.at[1])
-    upper = result.astype(jnp.bfloat16)
+    mine = dot(grad[:, near], right[...]) + dot(grad[:, far], held[1])
+    held[1] = mine.astype(jnp.bfloat16)
+    grad_sq[...] = jnp.broadcast_to(total(squared + squares(grad[...])), grad_sq.shape)
+
+
+def second_half(left, held, grad_sq, ratio, ready):
+    near, far = sides(left.shape[0])
+    yours = dot(held[2, :, near], held[1]) + dot(held[2, :, far], held[0])
+    squared = squares(yours)
+    ready()
+    mine = dot(left[:, near], held[1]) + dot(left[:, far], held[0])
+    squared = squared + squares(mine)
+    upper = mine.astype(jnp.bfloat16)
     held[0] = upper
-    held[1] = (result - upper.astype(f32)).astype(jnp.bfloat16)
-    cond_sq = squares(result) + squares(both(held.at[2], applied.at[0], applied.at[1]))
+    held[1] = (mine - upper.astype(f32)).astype(jnp.bfloat16)
     entries = BLK * BLK
-    grad_sq = jnp.sum(lane_sums(grad_sq), axis=1, keepdims=True)
-    cond_sq = jnp.sum(lane_sums(cond_sq), axis=1, keepdims=True)
-    ratio[...] = jnp.broadcast_to(
-        jnp.sqrt((grad_sq / entries + epsilon) / (cond_sq / entries + epsilon)), ratio.shape
+    ratio[...] = jnp.sqrt(
+        (grad_sq[...] / entries + epsilon) / (total(squared) / entries + epsilon)
     )
 
 
-def middle_kernel(plane, own, heard, sent, held, ratio, applied):
-    sent[...] = jnp.broadcast_to(jnp.sum(plane[...], axis=0, keepdims=True), sent.shape)
+def middle_kernel(plane, own, heard, sent, held, grad_sq, row, sem):
+    row[...] = jnp.broadcast_to(jnp.sum(plane[...], axis=0, keepdims=True), row.shape)
+    copy = pltpu.make_async_copy(row, sent, sem)
+    copy.start()
 
     @pl.when(lax.axis_index(LINE) < EARLY_PLANES)
     def _():
-        products(own, held, ratio, applied, lambda i: None)
-
-
-def late_kernel(grad, right, left, heard, held, ratio, applied, own, sems):
-    @pl.when(lax.axis_index(LINE) >= EARLY_PLANES)
+        first_half(own.at[0], own.at[1], held, grad_sq, lambda i: None)
+
+    copy.wait()
+
+
+def late_kernel(grad, right, left, heard, early_sq, held, ratio, own, grad_sq, sems):
+    load = pltpu.make_async_copy(left, own.at[2], sems.at[2])
+    load.start()
+    early = lax.axis_index(LINE) < EARLY_PLANES
+
+    @pl.when(jnp.logical_not(early))
     def _():
         copies = [
-            pltpu.make_async_copy(source, own.at[i], sems.at[i])
-            for i, source in enumerate((grad, right, left))
+            pltpu.make_async_copy(right, own.at[1], sems.at[1]),
+            pltpu.make_async_copy(grad, own.at[0], sems.at[0]),
         ]
-        for i in (1, 0, 2):
-            copies[i].start()
-        products(own, held, ratio, applied, lambda i: copies[i].wait())
+        for copy in copies:
+            copy.start()
+        first_half(own.at[0], own.at[1], held, grad_sq, lambda i: copies[i].wait())
+
+    @pl.when(early)
+    def _():
+        grad_sq[...] = early_sq[...]
+
+    second_half(own.at[2], held, grad_sq, ratio, load.wait)
 
 
 def middle(plane, own, heard, members):
-    _, rows, columns = heard.shape
     return pl.pallas_call(
         middle_kernel,
         out_shape=(
-            pltpu.VMEM((members, LANES), f32),
+            pltpu.HBM((members, LANES), f32),
             pltpu.VMEM(heard.shape, heard.dtype),
             pltpu.VMEM((8, LANES), f32),
         ),
         in_specs=[VMEM] * 3,
-        out_specs=(VMEM,) * 3,
+        out_specs=(HBM, VMEM, VMEM),
         input_output_aliases={2: 1},
-        scratch_shapes=[pltpu.VMEM((2, rows, columns), jnp.bfloat16)],
+        scratch_shapes=[pltpu.VMEM((members, LANES), f32), pltpu.SemaphoreType.DMA],
         compiler_params=pltpu.CompilerParams(vmem_limit_bytes=24 << 20),
         cost_estimate=pl.CostEstimate(flops=10**9, bytes_accessed=10**7, transcendentals=0),
         name="middle",
     )(plane, own, heard)
 
 
-def late(grad, right, left, heard):
-    _, rows, columns = heard.shape
+def late(grad, right, left, heard, early_sq):
     return pl.pallas_call(
         late_kernel,
         out_shape=(pltpu.VMEM(heard.shape, heard.dtype), pltpu.VMEM((8, LANES), f32)),
-        in_specs=[HBM, HBM, HBM, VMEM],
+        in_specs=[HBM, HBM, HBM, VMEM, VMEM],
         out_specs=(VMEM, VMEM),
         input_output_aliases={3: 0},
         scratch_shapes=[
-            pltpu.VMEM((2, rows, columns), jnp.bfloat16),
             pltpu.VMEM(heard.shape, heard.dtype),
+            pltpu.VMEM((8, LANES), f32),
             pltpu.SemaphoreType.DMA((3,)),
         ],
         compiler_params=pltpu.CompilerParams(vmem_limit_bytes=24 << 20),
         cost_estimate=pl.CostEstimate(flops=4 * 10**9, bytes_accessed=10**7, transcendentals=0),
         name="late",
-    )(grad, right, left, heard)
-
-
-def final_kernel(count, line, held, early_ratio, late_ratio, update, staged, sems):
+    )(grad, right, left, heard, early_sq)
+
+
+def final_kernel(count, line, held, ratio, update, staged, sems):
     rows = held.shape[1]
     step = rows // 4
-    total = jnp.sum(jnp.sum(line[...], axis=0, keepdims=True), axis=1, keepdims=True)
-    clip = clip_rms / jnp.sqrt(total / count + epsilon)
-    early = lax.axis_index(LINE) < EARLY_PLANES
-    scale = clip * jnp.where(early, early_ratio[0:1, 0:1], late_ratio[0:1, 0:1])
+    global_sq = jnp.sum(jnp.sum(line[...], axis=0, keepdims=True), axis=1, keepdims=True)
+    scale = clip_rms / jnp.sqrt(global_sq / count + epsilon) * ratio[0:1, 0:1]
     writes = []
     for i in range(4):
         piece = pl.ds(i * step, step)
@@ -204,12 +227,12 @@
         copy.wait()
 
 
-def final(count, line, held, early_ratio, late_ratio):
+def final(count, line, held, ratio):
     _, rows, columns = held.shape
     return pl.pallas_call(
         functools.partial(final_kernel, count),
         out_shape=jax.ShapeDtypeStruct((rows, columns), jnp.bfloat16),
-        in_specs=[VMEM] * 4,
+        in_specs=[VMEM] * 3,
         out_specs=HBM,
         scratch_shapes=[
             pltpu.VMEM((rows, columns), jnp.bfloat16),
@@ -217,7 +240,7 @@
         ],
         compiler_params=pltpu.CompilerParams(vmem_limit_bytes=16 << 20),
         name="final",
-    )(line, held, early_ratio, late_ratio)
+    )(line, held, ratio)
 
 
 def shards(grad, left_root, right_root):
@@ -229,11 +252,11 @@
         plane = tell_all(sent, PLANE, PLANE_FIRST)
     with jax.named_scope("exchange"):
         heard = partner(own, PLANE)
-    sent, held, early_ratio = middle(in_vmem(plane), own, heard, line_size)
+    sent, held, early_sq = middle(in_vmem(plane), own, heard, line_size)
     with jax.named_scope("line"):
         line = tell_all(sent, LINE, LINE_FIRST)
-    held, late_ratio = late(grad, right_root, left_root, held)
-    return final(count, in_vmem(line), held, early_ratio, late_ratio)
+    held, ratio = late(grad, right_root, left_root, held, early_sq)
+    return final(count, in_vmem(line), held, ratio)
 
 
 def solution(mesh):

time: 40.7 us -> 38.2 us (0.939)
  the two profiles are of different devices: /device:TPU:1 before, /device:TPU:2 now
where the time goes in v4:
time: 38.2 us; the launch traced here: 38 us
  blocking collectives  14.7 us (38%)
  starting transfers between devices  13.5 us (35%)
  Pallas kernels  8.34 us (22%)
  waiting for transfers between devices  1.38 us (4%)
    all_to_all x1, blocking collectives, tell_all(): lax.all_to_all(rows, axis, 0, 0, axis_index_groups=[group], tiled=True)  14.7 us
    all_to_all x1, starting transfers between devices, tell_all(): lax.all_to_all(rows, axis, 0, 0, axis_index_groups=[group], tiled=True)  11.6 us
    pallas_call x1, Pallas kernels, late(): pl.pallas_call(late_kernel, out_shape=(pltpu.VMEM(heard.shape, heard.dtyp...  2.77 us
    pallas_call x1, Pallas kernels, middle(): pl.pallas_call(middle_kernel, out_shape=(pltpu.HBM((members, LANES), f32)...  2.37 us
    ppermute x1, starting transfers between devices, partner(): lax.ppermute(shard, axis, [(i, i ^ 1) for i in range(lax.axis_size(axis))])  1.92 us
    pallas_call x1, Pallas kernels, head(): pl.pallas_call(head_kernel, out_shape=(pltpu.VMEM((3, rows, columns), gra...  1.92 us
    all_to_all x1, waiting for transfers between devices, tell_all(): lax.all_to_all(rows, axis, 0, 0, axis_index_groups=[group], tiled=True)  1.38 us
    pallas_call x1, Pallas kernels, final(): pl.pallas_call(functools.partial(final_kernel, count), out_shape=jax.Shap...  1.28 us
  transfers between devices with their start and end apart: 2, of which 1 were waited for; matrix products, arithmetic and copies ran while one was open for 0% of the time, Pallas kernels for 7%

profile of v4, /device:TPU:2, one launch (start us, length us, event | category | flops | bytes accessed | tf_op | source)
XLA Modules:
  0.0 38.0 jit_solution(12332056181200411974)
XLA Ops:
  0.0 1.9 %head.1 = (bf16[3,512,1024]{2,1,0:T(8,128)(2,1)S(1)}, f32[32,128]{1,0:T(8,128)S(1)}) custom-call(bf16[512,1024]{1,0:T(8,128)(2,1)} %grad.3, bf16[512,1024]{1,0:T(8,128)(2,1)} %left.3, bf16[512,1024]{1,0:T(8,128)(2,1)} %right.3), custom_call_target="tpu_custom_call" | custom-call | flops 1048576 | bytes 3145728 | tf_op jit(solution)/shard_map/head/pallas_call | solution.py:84
  1.9 1.9 %collective-permute-start = (bf16[3,512,1024]{2,1,0:T(8,128)(2,1)S(1)}, bf16[3,512,1024]{2,1,0:T(8,128)(2,1)S(1)}, u32[]{:S(2)}, u32[]{:S(2)}) collective-permute-start(bf16[3,512,1024]{2,1,0:T(8,128)(2,1)S(1)} %get-tuple-element.13.own), channel_id=1, source_target_pairs={{0,1},{1,0},{2,3},{3,2},{4,5},{5,4},{6,7},{7,6},{8,9},{9,8},{10,11... | collective-permute-start | bytes 9437192 | tf_op jit(solution)/shard_map/exchange/ppermute | solution.py:25
  3.9 14.7 %all_to_all.22 = f32[32,1,128]{2,1,0:T(1,128)S(1)} all-to-all(f32[32,1,128]{2,1,0:T(1,128)S(1)} %bitcast.10), channel_id=1, replica_groups={{11,12,13,14,15,16,17,18,19,20,21,22,23,24,25,26,27,28,29,30,31,0,1,2,3..., dimensions={0} | all-to-all | bytes 32768 | tf_op jit(solution)/shard_map/plane/all_to_all | solution.py:31
  18.5 0.0 collective-permute-done.heard
  18.5 2.4 %middle.1 = (f32[16,128]{1,0:T(8,128)}, bf16[3,512,1024]{2,1,0:T(8,128)(2,1)S(1)}, f32[8,128]{1,0:T(8,128)S(1)}) custom-call(f32[32,128]{1,0:T(8,128)S(1)} %bitcast.8, bf16[3,512,1024]{2,1,0:T(8,128)(2,1)S(1)} %get-tuple-element.13.own, bf16[3,512,1024]{2,1,0:T(8,128)(2,1)S(1)} %collective-permute-done.heard), custom_call_target="tpu_custom_call", output_to_operand_aliasing={{1}: (2, {})} | custom-call | flops 1000000000 | bytes 10000000 | tf_op jit(solution)/shard_map/middle/pallas_call | solution.py:179
  20.9 11.6 %all-to-all-start.1 = ((f32[16,1,128]{2,1,0:T(1,128)}), f32[16,1,128]{2,1,0:T(1,128)S(1)}, u32[]{:S(2)}, u32[]{:S(2)}) async-start(f32[16,1,128]{2,1,0:T(1,128)} %bitcast.11), calls=%async_computation.1 | async-start | bytes 16384 | tf_op jit(solution)/shard_map/line/all_to_all | solution.py:31
  32.5 2.8 %late.1 = (bf16[3,512,1024]{2,1,0:T(8,128)(2,1)S(1)}, f32[8,128]{1,0:T(8,128)S(1)}) custom-call(bf16[512,1024]{1,0:T(8,128)(2,1)} %grad.3, bf16[512,1024]{1,0:T(8,128)(2,1)} %right.3, bf16[512,1024]{1,0:T(8,128)(2,1)} %left.3, bf16[3,512,1024]{2,1,0:T(8,128)(2,1)S(1)} %get-tuple-element.15.heard, ...), custom_call_target="tpu_custom_call", output_to_operand_aliasing={{0}: (3, {})} | custom-call | flops 4000000000 | bytes 10000000 | tf_op jit(solution)/shard_map/late/pallas_call | solution.py:197
  35.3 1.4 %all-to-all-done.1 = f32[16,1,128]{2,1,0:T(1,128)S(1)} async-done(((f32[16,1,128]{2,1,0:T(1,128)}), f32[16,1,128]{2,1,0:T(1,128)S(1)}, u32[]{:S(2)}, u32[]{:S(2)}) %all-to-all-start.1) | async-done | bytes 8224 | tf_op jit(solution)/shard_map/line/all_to_all | solution.py:31
  36.7 1.3 %final.1 = bf16[512,1024]{1,0:T(8,128)(2,1)} custom-call(f32[16,128]{1,0:T(8,128)S(1)} %bitcast.9, bf16[3,512,1024]{2,1,0:T(8,128)(2,1)S(1)} %get-tuple-element.17.held, f32[8,128]{1,0:T(8,128)S(1)} %get-tuple-element.18.ratio), custom_call_target="tpu_custom_call" | custom-call | tf_op jit(solution)/shard_map/final/pallas_call | solution.py:232
Async XLA Ops:
  1.9 16.6 %collective-permute-start = (bf16[3,512,1024]{2,1,0:T(8,128)(2,1)S(1)}, bf16[3,512,1024]{2,1,0:T(8,128)(2,1)S(1)}, u32[]{:S(2)}, u32[]{:S(2)}) collective-permute-start(bf16[3,512,1024]{2,1,0:T(8,128)(2,1)S(1)} %get-tuple-element.13.own), channel_id=1, source_target_pairs={{0,1},{1,0},{2,3},{3,2},{4,5},{5,4},{6,7},{7,6},{8,9},{9,8},{10,11... | collective-permute-start | bytes 9437192 | tf_op jit(solution)/shard_map/exchange/ppermute | solution.py:25
  20.9 15.8 %all-to-all-start.1 = ((f32[16,1,128]{2,1,0:T(1,128)}), f32[16,1,128]{2,1,0:T(1,128)S(1)}, u32[]{:S(2)}, u32[]{:S(2)}) async-start(f32[16,1,128]{2,1,0:T(1,128)} %bitcast.11), calls=%async_computation.1 | async-start | bytes 16384 | tf_op jit(solution)/shard_map/line/all_to_all | solution.py:31

commit v5 on v4

--- a/solution.py
+++ b/solution.py
@@ -9,8 +9,9 @@
 from jax.sharding import PartitionSpec as P
 
 BLK = 1024
-LINE, PLANE = "line", "plane"
-ALL = (LINE, PLANE)
+DEV = "dev"
+PLANES = 16
+SWAPPED_PLANES = (10,)
 LINE_FIRST = 10
 PLANE_FIRST = 11
 EARLY_PLANES = 4
@@ -25,10 +26,22 @@
     return lax.ppermute(shard, axis, [(i, i ^ 1) for i in range(lax.axis_size(axis))])
 
 
-def tell_all(rows, axis, first):
-    members = lax.axis_size(axis)
-    group = [(first + i) % members for i in range(members)]
-    return lax.all_to_all(rows, axis, 0, 0, axis_index_groups=[group], tiled=True)
+def tell_all(rows, groups):
+    return lax.all_to_all(rows, DEV, 0, 0, axis_index_groups=groups, tiled=True)
+
+
+def plane_groups(planes, across):
+    order = [(PLANE_FIRST + i) % across for i in range(across)]
+    return [[z * across + i for i in order] for z in range(planes)]
+
+
+def line_groups(planes, across):
+    order = [(LINE_FIRST + z) % planes for z in range(planes)]
+
+    def place(z, i):
+        return z * across + (i ^ 1 if z in SWAPPED_PLANES and i > 1 else i)
+
+    return [[place(z, i) for z in order] for i in range(across)]
 
 
 def in_hbm(array):
@@ -99,7 +112,7 @@
 
 
 def sides(rows):
-    parity = lax.axis_index(PLANE) % 2
+    parity = lax.axis_index(DEV) % 2
     near = pl.ds(pl.multiple_of(parity * rows, rows), rows)
     far = pl.ds(pl.multiple_of((1 - parity) * rows, rows), rows)
     return near, far
@@ -146,7 +159,7 @@
     copy = pltpu.make_async_copy(row, sent, sem)
     copy.start()
 
-    @pl.when(lax.axis_index(LINE) < EARLY_PLANES)
+    @pl.when(lax.axis_index(DEV) < EARLY_PLANES * (lax.axis_size(DEV) // PLANES))
     def _():
         first_half(own.at[0], own.at[1], held, grad_sq, lambda i: None)
 
@@ -156,7 +169,7 @@
 def late_kernel(grad, right, left, heard, early_sq, held, ratio, own, grad_sq, sems):
     load = pltpu.make_async_copy(left, own.at[2], sems.at[2])
     load.start()
-    early = lax.axis_index(LINE) < EARLY_PLANES
+    early = lax.axis_index(DEV) < EARLY_PLANES * (lax.axis_size(DEV) // PLANES)
 
     @pl.when(jnp.logical_not(early))
     def _():
@@ -213,11 +226,11 @@
 
 def final_kernel(count, line, held, ratio, update, staged, sems):
     rows = held.shape[1]
-    step = rows // 4
+    step = rows // 8
     global_sq = jnp.sum(jnp.sum(line[...], axis=0, keepdims=True), axis=1, keepdims=True)
     scale = clip_rms / jnp.sqrt(global_sq / count + epsilon) * ratio[0:1, 0:1]
     writes = []
-    for i in range(4):
+    for i in range(8):
         piece = pl.ds(i * step, step)
         result = held[0, piece, :].astype(f32) + held[1, piece, :].astype(f32)
         staged[piece, :] = (scale * result).astype(jnp.bfloat16)
@@ -236,7 +249,7 @@
         out_specs=HBM,
         scratch_shapes=[
             pltpu.VMEM((rows, columns), jnp.bfloat16),
-            pltpu.SemaphoreType.DMA((4,)),
+            pltpu.SemaphoreType.DMA((8,)),
         ],
         compiler_params=pltpu.CompilerParams(vmem_limit_bytes=16 << 20),
         name="final",
@@ -244,27 +257,27 @@
 
 
 def shards(grad, left_root, right_root):
-    plane_size, line_size = lax.axis_size(PLANE), lax.axis_size(LINE)
+    plane_size, line_size = lax.axis_size(DEV) // PLANES, PLANES
     count = float(plane_size * line_size // 2 * BLK * BLK)
     grad, left_root, right_root = (in_hbm(x) for x in (grad, left_root, right_root))
     own, sent = head(grad, left_root, right_root, plane_size)
     with jax.named_scope("plane"):
-        plane = tell_all(sent, PLANE, PLANE_FIRST)
+        plane = tell_all(sent, plane_groups(line_size, plane_size))
     with jax.named_scope("exchange"):
-        heard = partner(own, PLANE)
+        heard = partner(own, DEV)
     sent, held, early_sq = middle(in_vmem(plane), own, heard, line_size)
     with jax.named_scope("line"):
-        line = tell_all(sent, LINE, LINE_FIRST)
+        line = tell_all(sent, line_groups(line_size, plane_size))
     held, ratio = late(grad, right_root, left_root, held, early_sq)
     return final(count, in_vmem(line), held, ratio)
 
 
 def solution(mesh):
-    torus = Mesh(mesh.devices.reshape(16, 32), ALL)
+    torus = Mesh(mesh.devices.reshape(mesh.size), (DEV,))
     return jax.shard_map(
         shards,
         mesh=torus,
-        in_specs=(P(ALL, None), P(ALL, None), P(ALL, None)),
-        out_specs=P(ALL, None),
+        in_specs=(P(DEV, None), P(DEV, None), P(DEV, None)),
+        out_specs=P(DEV, None),
         check_vma=False,
     )

time: 38.2 us -> 37.8 us (0.990)
  the two profiles are of different devices: /device:TPU:2 before, /device:TPU:1 now
where the time goes in v5:
time: 37.8 us; the launch traced here: 37.2 us
  starting transfers between devices  19.8 us (52%)
  blocking collectives  8.62 us (23%)
  Pallas kernels  8.25 us (22%)
  waiting for transfers between devices  0.51 us (1%)
    all_to_all x1, starting transfers between devices, tell_all(): return lax.all_to_all(rows, DEV, 0, 0, axis_index_groups=groups, tiled=True)  11 us
    ppermute x1, starting transfers between devices, partner(): lax.ppermute(shard, axis, [(i, i ^ 1) for i in range(lax.axis_size(axis))])  8.75 us
    all_to_all x1, blocking collectives, tell_all(): return lax.all_to_all(rows, DEV, 0, 0, axis_index_groups=groups, tiled=True)  8.62 us
    pallas_call x1, Pallas kernels, late(): pl.pallas_call(late_kernel, out_shape=(pltpu.VMEM(heard.shape, heard.dtyp...  2.77 us
    pallas_call x1, Pallas kernels, middle(): pl.pallas_call(middle_kernel, out_shape=(pltpu.HBM((members, LANES), f32)...  2.37 us
    pallas_call x1, Pallas kernels, head(): pl.pallas_call(head_kernel, out_shape=(pltpu.VMEM((3, rows, columns), gra...  1.92 us
    pallas_call x1, Pallas kernels, final(): pl.pallas_call(functools.partial(final_kernel, count), out_shape=jax.Shap...  1.19 us
  transfers between devices with their start and end apart: 2, of which 1 were waited for; matrix products, arithmetic and copies ran while one was open for 0% of the time, Pallas kernels for 7%

profile of v5, /device:TPU:1, one launch (start us, length us, event | category | flops | bytes accessed | tf_op | source)
XLA Modules:
  0.0 37.2 jit_solution(8830675823112763346)
XLA Ops:
  0.0 1.9 %head.1 = (bf16[3,512,1024]{2,1,0:T(8,128)(2,1)S(1)}, f32[32,128]{1,0:T(8,128)S(1)}) custom-call(bf16[512,1024]{1,0:T(8,128)(2,1)} %grad.3, bf16[512,1024]{1,0:T(8,128)(2,1)} %left.3, bf16[512,1024]{1,0:T(8,128)(2,1)} %right.3), custom_call_target="tpu_custom_call" | custom-call | flops 1048576 | bytes 3145728 | tf_op jit(solution)/shard_map/head/pallas_call | solution.py:97
  1.9 8.7 %collective-permute-start = (bf16[3,512,1024]{2,1,0:T(8,128)(2,1)S(1)}, bf16[3,512,1024]{2,1,0:T(8,128)(2,1)S(1)}, u32[]{:S(2)}, u32[]{:S(2)}) collective-permute-start(bf16[3,512,1024]{2,1,0:T(8,128)(2,1)S(1)} %get-tuple-element.13.own), channel_id=1, source_target_pairs={{0,1},{1,0},{2,3},{3,2},{4,5},{5,4},{6,7},{7,6},{8,9},{9,8},{10,11... | collective-permute-start | bytes 9437192 | tf_op jit(solution)/shard_map/exchange/ppermute | solution.py:26
  10.7 8.6 %all_to_all.22 = f32[32,1,128]{2,1,0:T(1,128)S(1)} all-to-all(f32[32,1,128]{2,1,0:T(1,128)S(1)} %bitcast.10), channel_id=1, replica_groups={{11,12,13,14,15,16,17,18,19,20,21,22,23,24,25,26,27,28,29,30,31,0,1,2,3..., dimensions={0} | all-to-all | bytes 32768 | tf_op jit(solution)/shard_map/plane/all_to_all | solution.py:30
  19.3 0.0 collective-permute-done.heard
  19.3 2.4 %middle.1 = (f32[16,128]{1,0:T(8,128)}, bf16[3,512,1024]{2,1,0:T(8,128)(2,1)S(1)}, f32[8,128]{1,0:T(8,128)S(1)}) custom-call(f32[32,128]{1,0:T(8,128)S(1)} %bitcast.8, bf16[3,512,1024]{2,1,0:T(8,128)(2,1)S(1)} %get-tuple-element.13.own, bf16[3,512,1024]{2,1,0:T(8,128)(2,1)S(1)} %collective-permute-done.heard), custom_call_target="tpu_custom_call", output_to_operand_aliasing={{1}: (2, {})} | custom-call | flops 1000000000 | bytes 10000000 | tf_op jit(solution)/shard_map/middle/pallas_call | solution.py:192
  21.7 11.0 %all-to-all-start.1 = ((f32[16,1,128]{2,1,0:T(1,128)}), f32[16,1,128]{2,1,0:T(1,128)S(1)}, u32[]{:S(2)}, u32[]{:S(2)}) async-start(f32[16,1,128]{2,1,0:T(1,128)} %bitcast.11), calls=%async_computation.1 | async-start | bytes 16384 | tf_op jit(solution)/shard_map/line/all_to_all | solution.py:30
  32.7 2.8 %late.1 = (bf16[3,512,1024]{2,1,0:T(8,128)(2,1)S(1)}, f32[8,128]{1,0:T(8,128)S(1)}) custom-call(bf16[512,1024]{1,0:T(8,128)(2,1)} %grad.3, bf16[512,1024]{1,0:T(8,128)(2,1)} %right.3, bf16[512,1024]{1,0:T(8,128)(2,1)} %left.3, bf16[3,512,1024]{2,1,0:T(8,128)(2,1)S(1)} %get-tuple-element.15.heard, ...), custom_call_target="tpu_custom_call", output_to_operand_aliasing={{0}: (3, {})} | custom-call | flops 4000000000 | bytes 10000000 | tf_op jit(solution)/shard_map/late/pallas_call | solution.py:210
  35.5 0.5 %all-to-all-done.1 = f32[16,1,128]{2,1,0:T(1,128)S(1)} async-done(((f32[16,1,128]{2,1,0:T(1,128)}), f32[16,1,128]{2,1,0:T(1,128)S(1)}, u32[]{:S(2)}, u32[]{:S(2)}) %all-to-all-start.1) | async-done | bytes 8224 | tf_op jit(solution)/shard_map/line/all_to_all | solution.py:30
  36.0 1.2 %final.1 = bf16[512,1024]{1,0:T(8,128)(2,1)} custom-call(f32[16,128]{1,0:T(8,128)S(1)} %bitcast.9, bf16[3,512,1024]{2,1,0:T(8,128)(2,1)S(1)} %get-tuple-element.17.held, f32[8,128]{1,0:T(8,128)S(1)} %get-tuple-element.18.ratio), custom_call_target="tpu_custom_call" | custom-call | tf_op jit(solution)/shard_map/final/pallas_call | solution.py:245
Async XLA Ops:
  1.9 17.4 %collective-permute-start = (bf16[3,512,1024]{2,1,0:T(8,128)(2,1)S(1)}, bf16[3,512,1024]{2,1,0:T(8,128)(2,1)S(1)}, u32[]{:S(2)}, u32[]{:S(2)}) collective-permute-start(bf16[3,512,1024]{2,1,0:T(8,128)(2,1)S(1)} %get-tuple-element.13.own), channel_id=1, source_target_pairs={{0,1},{1,0},{2,3},{3,2},{4,5},{5,4},{6,7},{7,6},{8,9},{9,8},{10,11... | collective-permute-start | bytes 9437192 | tf_op jit(solution)/shard_map/exchange/ppermute | solution.py:26
  21.7 14.3 %all-to-all-start.1 = ((f32[16,1,128]{2,1,0:T(1,128)}), f32[16,1,128]{2,1,0:T(1,128)S(1)}, u32[]{:S(2)}, u32[]{:S(2)}) async-start(f32[16,1,128]{2,1,0:T(1,128)} %bitcast.11), calls=%async_computation.1 | async-start | bytes 16384 | tf_op jit(solution)/shard_map/line/all_to_all | solution.py:30

commit v6 on v5

--- a/solution.py
+++ b/solution.py
@@ -11,8 +11,8 @@
 BLK = 1024
 DEV = "dev"
 PLANES = 16
-SWAPPED_PLANES = (10,)
-LINE_FIRST = 10
+SWAPPED_PLANES = (11, 15)
+LINE_FIRST = 11
 PLANE_FIRST = 11
 EARLY_PLANES = 4
 LANES = 128

time: 37.8 us -> 37.5 us (level)
  starting transfers between devices: 19.8 us -> 18.9 us
  waiting for transfers between devices: 0.51 us -> 1.41 us
    all_to_all x1, waiting for transfers between devices: 0.51 us -> 1.41 us  [tell_all(): return lax.all_to_all(rows, DEV, 0, 0, axis_index_groups=groups, tiled=True)]
    all_to_all x1, starting transfers between devices: 11 us -> 10.1 us  [tell_all(): return lax.all_to_all(rows, DEV, 0, 0, axis_index_groups=groups, tiled=True)]
where the time goes in v6:
time: 37.5 us; the launch traced here: 37.2 us
  starting transfers between devices  18.9 us (50%)
  blocking collectives  8.62 us (23%)
  Pallas kernels  8.25 us (22%)
  waiting for transfers between devices  1.41 us (4%)
    all_to_all x1, starting transfers between devices, tell_all(): return lax.all_to_all(rows, DEV, 0, 0, axis_index_groups=groups, tiled=True)  10.1 us
    ppermute x1, starting transfers between devices, partner(): lax.ppermute(shard, axis, [(i, i ^ 1) for i in range(lax.axis_size(axis))])  8.75 us
    all_to_all x1, blocking collectives, tell_all(): return lax.all_to_all(rows, DEV, 0, 0, axis_index_groups=groups, tiled=True)  8.62 us
    pallas_call x1, Pallas kernels, late(): pl.pallas_call(late_kernel, out_shape=(pltpu.VMEM(heard.shape, heard.dtyp...  2.77 us
    pallas_call x1, Pallas kernels, middle(): pl.pallas_call(middle_kernel, out_shape=(pltpu.HBM((members, LANES), f32)...  2.37 us
    pallas_call x1, Pallas kernels, head(): pl.pallas_call(head_kernel, out_shape=(pltpu.VMEM((3, rows, columns), gra...  1.92 us
    all_to_all x1, waiting for transfers between devices, tell_all(): return lax.all_to_all(rows, DEV, 0, 0, axis_index_groups=groups, tiled=True)  1.41 us
    pallas_call x1, Pallas kernels, final(): pl.pallas_call(functools.partial(final_kernel, count), out_shape=jax.Shap...  1.19 us
  transfers between devices with their start and end apart: 2, of which 1 were waited for; matrix products, arithmetic and copies ran while one was open for 0% of the time, Pallas kernels for 7%

profile of v6, /device:TPU:1, one launch (start us, length us, event | category | flops | bytes accessed | tf_op | source)
XLA Modules:
  0.0 37.2 jit_solution(13308282949025515549)
XLA Ops:
  0.0 1.9 %head.1 = (bf16[3,512,1024]{2,1,0:T(8,128)(2,1)S(1)}, f32[32,128]{1,0:T(8,128)S(1)}) custom-call(bf16[512,1024]{1,0:T(8,128)(2,1)} %grad.3, bf16[512,1024]{1,0:T(8,128)(2,1)} %left.3, bf16[512,1024]{1,0:T(8,128)(2,1)} %right.3), custom_call_target="tpu_custom_call" | custom-call | flops 1048576 | bytes 3145728 | tf_op jit(solution)/shard_map/head/pallas_call | solution.py:97
  1.9 8.7 %collective-permute-start = (bf16[3,512,1024]{2,1,0:T(8,128)(2,1)S(1)}, bf16[3,512,1024]{2,1,0:T(8,128)(2,1)S(1)}, u32[]{:S(2)}, u32[]{:S(2)}) collective-permute-start(bf16[3,512,1024]{2,1,0:T(8,128)(2,1)S(1)} %get-tuple-element.13.own), channel_id=1, source_target_pairs={{0,1},{1,0},{2,3},{3,2},{4,5},{5,4},{6,7},{7,6},{8,9},{9,8},{10,11... | collective-permute-start | bytes 9437192 | tf_op jit(solution)/shard_map/exchange/ppermute | solution.py:26
  10.7 8.6 %all_to_all.22 = f32[32,1,128]{2,1,0:T(1,128)S(1)} all-to-all(f32[32,1,128]{2,1,0:T(1,128)S(1)} %bitcast.10), channel_id=1, replica_groups={{11,12,13,14,15,16,17,18,19,20,21,22,23,24,25,26,27,28,29,30,31,0,1,2,3..., dimensions={0} | all-to-all | bytes 32768 | tf_op jit(solution)/shard_map/plane/all_to_all | solution.py:30
  19.3 0.0 collective-permute-done.heard
  19.3 2.4 %middle.1 = (f32[16,128]{1,0:T(8,128)}, bf16[3,512,1024]{2,1,0:T(8,128)(2,1)S(1)}, f32[8,128]{1,0:T(8,128)S(1)}) custom-call(f32[32,128]{1,0:T(8,128)S(1)} %bitcast.8, bf16[3,512,1024]{2,1,0:T(8,128)(2,1)S(1)} %get-tuple-element.13.own, bf16[3,512,1024]{2,1,0:T(8,128)(2,1)S(1)} %collective-permute-done.heard), custom_call_target="tpu_custom_call", output_to_operand_aliasing={{1}: (2, {})} | custom-call | flops 1000000000 | bytes 10000000 | tf_op jit(solution)/shard_map/middle/pallas_call | solution.py:192
  21.7 10.1 %all-to-all-start.1 = ((f32[16,1,128]{2,1,0:T(1,128)}), f32[16,1,128]{2,1,0:T(1,128)S(1)}, u32[]{:S(2)}, u32[]{:S(2)}) async-start(f32[16,1,128]{2,1,0:T(1,128)} %bitcast.11), calls=%async_computation.1 | async-start | bytes 16384 | tf_op jit(solution)/shard_map/line/all_to_all | solution.py:30
  31.8 2.8 %late.1 = (bf16[3,512,1024]{2,1,0:T(8,128)(2,1)S(1)}, f32[8,128]{1,0:T(8,128)S(1)}) custom-call(bf16[512,1024]{1,0:T(8,128)(2,1)} %grad.3, bf16[512,1024]{1,0:T(8,128)(2,1)} %right.3, bf16[512,1024]{1,0:T(8,128)(2,1)} %left.3, bf16[3,512,1024]{2,1,0:T(8,128)(2,1)S(1)} %get-tuple-element.15.heard, ...), custom_call_target="tpu_custom_call", output_to_operand_aliasing={{0}: (3, {})} | custom-call | flops 4000000000 | bytes 10000000 | tf_op jit(solution)/shard_map/late/pallas_call | solution.py:210
  34.6 1.4 %all-to-all-done.1 = f32[16,1,128]{2,1,0:T(1,128)S(1)} async-done(((f32[16,1,128]{2,1,0:T(1,128)}), f32[16,1,128]{2,1,0:T(1,128)S(1)}, u32[]{:S(2)}, u32[]{:S(2)}) %all-to-all-start.1) | async-done | bytes 8224 | tf_op jit(solution)/shard_map/line/all_to_all | solution.py:30
  36.0 1.2 %final.1 = bf16[512,1024]{1,0:T(8,128)(2,1)} custom-call(f32[16,128]{1,0:T(8,128)S(1)} %bitcast.9, bf16[3,512,1024]{2,1,0:T(8,128)(2,1)S(1)} %get-tuple-element.17.held, f32[8,128]{1,0:T(8,128)S(1)} %get-tuple-element.18.ratio), custom_call_target="tpu_custom_call" | custom-call | tf_op jit(solution)/shard_map/final/pallas_call | solution.py:245
Async XLA Ops:
  1.9 17.4 %collective-permute-start = (bf16[3,512,1024]{2,1,0:T(8,128)(2,1)S(1)}, bf16[3,512,1024]{2,1,0:T(8,128)(2,1)S(1)}, u32[]{:S(2)}, u32[]{:S(2)}) collective-permute-start(bf16[3,512,1024]{2,1,0:T(8,128)(2,1)S(1)} %get-tuple-element.13.own), channel_id=1, source_target_pairs={{0,1},{1,0},{2,3},{3,2},{4,5},{5,4},{6,7},{7,6},{8,9},{9,8},{10,11... | collective-permute-start | bytes 9437192 | tf_op jit(solution)/shard_map/exchange/ppermute | solution.py:26
  21.7 14.3 %all-to-all-start.1 = ((f32[16,1,128]{2,1,0:T(1,128)}), f32[16,1,128]{2,1,0:T(1,128)S(1)}, u32[]{:S(2)}, u32[]{:S(2)}) async-start(f32[16,1,128]{2,1,0:T(1,128)} %bitcast.11), calls=%async_computation.1 | async-start | bytes 16384 | tf_op jit(solution)/shard_map/line/all_to_all | solution.py:30

commit v7 on v6

--- a/solution.py
+++ b/solution.py
@@ -226,12 +226,12 @@
 
 def final_kernel(count, line, held, ratio, update, staged, sems):
     rows = held.shape[1]
-    step = rows // 8
     global_sq = jnp.sum(jnp.sum(line[...], axis=0, keepdims=True), axis=1, keepdims=True)
-    scale = clip_rms / jnp.sqrt(global_sq / count + epsilon) * ratio[0:1, 0:1]
+    scale = clip_rms * lax.rsqrt(global_sq / count + epsilon) * ratio[0:1, 0:1]
     writes = []
-    for i in range(8):
-        piece = pl.ds(i * step, step)
+    edges = [0, 1, 2, 4, 6, 8, 10, 12, 14, 15, 16]
+    for i, (start, stop) in enumerate(zip(edges, edges[1:])):
+        piece = pl.ds(start * rows // 16, (stop - start) * rows // 16)
         result = held[0, piece, :].astype(f32) + held[1, piece, :].astype(f32)
         staged[piece, :] = (scale * result).astype(jnp.bfloat16)
         writes.append(pltpu.make_async_copy(staged.at[piece], update.at[piece], sems.at[i]))
@@ -249,7 +249,7 @@
         out_specs=HBM,
         scratch_shapes=[
             pltpu.VMEM((rows, columns), jnp.bfloat16),
-            pltpu.SemaphoreType.DMA((8,)),
+            pltpu.SemaphoreType.DMA((10,)),
         ],
         compiler_params=pltpu.CompilerParams(vmem_limit_bytes=16 << 20),
         name="final",

time: 37.5 us -> 37.5 us (level)
  no operation moved by 1% of the time
where the time goes in v7:
time: 37.5 us; the launch traced here: 37.2 us
  starting transfers between devices  18.9 us (50%)
  blocking collectives  8.62 us (23%)
  Pallas kernels  8.24 us (22%)
  waiting for transfers between devices  1.41 us (4%)
    all_to_all x1, starting transfers between devices, tell_all(): return lax.all_to_all(rows, DEV, 0, 0, axis_index_groups=groups, tiled=True)  10.1 us
    ppermute x1, starting transfers between devices, partner(): lax.ppermute(shard, axis, [(i, i ^ 1) for i in range(lax.axis_size(axis))])  8.75 us
    all_to_all x1, blocking collectives, tell_all(): return lax.all_to_all(rows, DEV, 0, 0, axis_index_groups=groups, tiled=True)  8.62 us
    pallas_call x1, Pallas kernels, late(): pl.pallas_call(late_kernel, out_shape=(pltpu.VMEM(heard.shape, heard.dtyp...  2.77 us
    pallas_call x1, Pallas kernels, middle(): pl.pallas_call(middle_kernel, out_shape=(pltpu.HBM((members, LANES), f32)...  2.37 us
    pallas_call x1, Pallas kernels, head(): pl.pallas_call(head_kernel, out_shape=(pltpu.VMEM((3, rows, columns), gra...  1.92 us
    all_to_all x1, waiting for transfers between devices, tell_all(): return lax.all_to_all(rows, DEV, 0, 0, axis_index_groups=groups, tiled=True)  1.41 us
    pallas_call x1, Pallas kernels, final(): pl.pallas_call(functools.partial(final_kernel, count), out_shape=jax.Shap...  1.19 us
  transfers between devices with their start and end apart: 2, of which 1 were waited for; matrix products, arithmetic and copies ran while one was open for 0% of the time, Pallas kernels for 7%

profile of v7, /device:TPU:1, one launch (start us, length us, event | category | flops | bytes accessed | tf_op | source)
XLA Modules:
  0.0 37.2 jit_solution(5131636750249115171)
XLA Ops:
  0.0 1.9 %head.1 = (bf16[3,512,1024]{2,1,0:T(8,128)(2,1)S(1)}, f32[32,128]{1,0:T(8,128)S(1)}) custom-call(bf16[512,1024]{1,0:T(8,128)(2,1)} %grad.3, bf16[512,1024]{1,0:T(8,128)(2,1)} %left.3, bf16[512,1024]{1,0:T(8,128)(2,1)} %right.3), custom_call_target="tpu_custom_call" | custom-call | flops 1048576 | bytes 3145728 | tf_op jit(solution)/shard_map/head/pallas_call | solution.py:97
  1.9 8.7 %collective-permute-start = (bf16[3,512,1024]{2,1,0:T(8,128)(2,1)S(1)}, bf16[3,512,1024]{2,1,0:T(8,128)(2,1)S(1)}, u32[]{:S(2)}, u32[]{:S(2)}) collective-permute-start(bf16[3,512,1024]{2,1,0:T(8,128)(2,1)S(1)} %get-tuple-element.13.own), channel_id=1, source_target_pairs={{0,1},{1,0},{2,3},{3,2},{4,5},{5,4},{6,7},{7,6},{8,9},{9,8},{10,11... | collective-permute-start | bytes 9437192 | tf_op jit(solution)/shard_map/exchange/ppermute | solution.py:26
  10.7 8.6 %all_to_all.22 = f32[32,1,128]{2,1,0:T(1,128)S(1)} all-to-all(f32[32,1,128]{2,1,0:T(1,128)S(1)} %bitcast.10), channel_id=1, replica_groups={{11,12,13,14,15,16,17,18,19,20,21,22,23,24,25,26,27,28,29,30,31,0,1,2,3..., dimensions={0} | all-to-all | bytes 32768 | tf_op jit(solution)/shard_map/plane/all_to_all | solution.py:30
  19.3 0.0 collective-permute-done.heard
  19.3 2.4 %middle.1 = (f32[16,128]{1,0:T(8,128)}, bf16[3,512,1024]{2,1,0:T(8,128)(2,1)S(1)}, f32[8,128]{1,0:T(8,128)S(1)}) custom-call(f32[32,128]{1,0:T(8,128)S(1)} %bitcast.8, bf16[3,512,1024]{2,1,0:T(8,128)(2,1)S(1)} %get-tuple-element.13.own, bf16[3,512,1024]{2,1,0:T(8,128)(2,1)S(1)} %collective-permute-done.heard), custom_call_target="tpu_custom_call", output_to_operand_aliasing={{1}: (2, {})} | custom-call | flops 1000000000 | bytes 10000000 | tf_op jit(solution)/shard_map/middle/pallas_call | solution.py:192
  21.7 10.1 %all-to-all-start.1 = ((f32[16,1,128]{2,1,0:T(1,128)}), f32[16,1,128]{2,1,0:T(1,128)S(1)}, u32[]{:S(2)}, u32[]{:S(2)}) async-start(f32[16,1,128]{2,1,0:T(1,128)} %bitcast.11), calls=%async_computation.1 | async-start | bytes 16384 | tf_op jit(solution)/shard_map/line/all_to_all | solution.py:30
  31.8 2.8 %late.1 = (bf16[3,512,1024]{2,1,0:T(8,128)(2,1)S(1)}, f32[8,128]{1,0:T(8,128)S(1)}) custom-call(bf16[512,1024]{1,0:T(8,128)(2,1)} %grad.3, bf16[512,1024]{1,0:T(8,128)(2,1)} %right.3, bf16[512,1024]{1,0:T(8,128)(2,1)} %left.3, bf16[3,512,1024]{2,1,0:T(8,128)(2,1)S(1)} %get-tuple-element.15.heard, ...), custom_call_target="tpu_custom_call", output_to_operand_aliasing={{0}: (3, {})} | custom-call | flops 4000000000 | bytes 10000000 | tf_op jit(solution)/shard_map/late/pallas_call | solution.py:210
  34.6 1.4 %all-to-all-done.1 = f32[16,1,128]{2,1,0:T(1,128)S(1)} async-done(((f32[16,1,128]{2,1,0:T(1,128)}), f32[16,1,128]{2,1,0:T(1,128)S(1)}, u32[]{:S(2)}, u32[]{:S(2)}) %all-to-all-start.1) | async-done | bytes 8224 | tf_op jit(solution)/shard_map/line/all_to_all | solution.py:30
  36.0 1.2 %final.1 = bf16[512,1024]{1,0:T(8,128)(2,1)} custom-call(f32[16,128]{1,0:T(8,128)S(1)} %bitcast.9, bf16[3,512,1024]{2,1,0:T(8,128)(2,1)S(1)} %get-tuple-element.17.held, f32[8,128]{1,0:T(8,128)S(1)} %get-tuple-element.18.ratio), custom_call_target="tpu_custom_call" | custom-call | tf_op jit(solution)/shard_map/final/pallas_call | solution.py:245
Async XLA Ops:
  1.9 17.4 %collective-permute-start = (bf16[3,512,1024]{2,1,0:T(8,128)(2,1)S(1)}, bf16[3,512,1024]{2,1,0:T(8,128)(2,1)S(1)}, u32[]{:S(2)}, u32[]{:S(2)}) collective-permute-start(bf16[3,512,1024]{2,1,0:T(8,128)(2,1)S(1)} %get-tuple-element.13.own), channel_id=1, source_target_pairs={{0,1},{1,0},{2,3},{3,2},{4,5},{5,4},{6,7},{7,6},{8,9},{9,8},{10,11... | collective-permute-start | bytes 9437192 | tf_op jit(solution)/shard_map/exchange/ppermute | solution.py:26
  21.7 14.3 %all-to-all-start.1 = ((f32[16,1,128]{2,1,0:T(1,128)}), f32[16,1,128]{2,1,0:T(1,128)S(1)}, u32[]{:S(2)}, u32[]{:S(2)}) async-start(f32[16,1,128]{2,1,0:T(1,128)} %bitcast.11), calls=%async_computation.1 | async-start | bytes 16384 | tf_op jit(solution)/shard_map/line/all_to_all | solution.py:30
